TPU v7x, 256 devices: a whole 4x4x8 slice. The times are simulated.
256 devices in a mesh: dom: 256 (over y, x, z, core).
Axes of the slice: x: 4, y: 4, z: 8, core: 2. Of those that a mesh axis runs over, the one named last changes fastest.
Arguments:
- displacement: float32 [8, 3, 524288], P(None, None, 'dom'), may hold values from -1.5 to 1.5
- adjoint_disp: float32 [8, 3, 524288], P(None, None, 'dom'), may hold values from -1.5 to 1.5
- pressure: float32 [8, 524288], P(None, 'dom'), may hold values from -3 to 3
- adjoint_pressure: float32 [8, 524288], P(None, 'dom'), may hold values from -3 to 3
- youngs: float32 [524288], P('dom'), may hold values from 0.5 to 2
- permeability: float32 [524288], P('dom'), may hold values from 0.3 to 3
- stiffness: float32 [24, 24], replicated
- send_nodes: int32 [8, 32768], P(None, 'dom'), may hold values from 0 to 2047
- send_cells: int32 [8, 32768], P(None, 'dom'), may hold values from 0 to 2047
- elem_nodes: int32 [8, 524288], P(None, 'dom'), may hold values from 0 to 3071, as said below
- inner_faces: int32 [2, 1572864], P(None, 'dom'), may hold values from 0 to 2047
- cross_faces: int32 [2, 262144], P(None, 'dom'), may hold values from 0 to 2047, as said below
Outputs:
- grad_log_youngs: float32 [524288], P('dom')
- grad_log_perm: float32 [524288], P('dom')
Inputs may be any that keep to these rules, and one draw needn't show every extreme that they name: `send_cells`: entries refer to the partition's own cells; block j of partition c is read by partition c - o_j. `elem_nodes`: The first 1536 elements of each partition name only its own nodes; corner 0 of each of the last 512 is a ghost node. `cross_faces`: row 0 is an own cell; row 1 is j * 128 + g with d + o_j always on the axis. `inner_faces`: both rows name cells of the same partition.
All inputs are finite; a program needn't handle non-finite values.
Results may differ from a plain program's by a relative error of at most 0.0003.
Values sent between devices are 32-bit elements; how exact they have to be, the bound alone decides.
A program may use at most 192 MiB of HBM per device.

v0:
```python
import math

import jax
import jax.numpy as jnp
from jax import lax
from jax.sharding import PartitionSpec as P

OFFSETS = (1, -1, 2, -2, 4, -4, 8, -8)


def shifted(value, axis, steps):
    count = lax.axis_size(axis)
    leading, last = (max(0, -steps), min(count, count - steps))
    return lax.ppermute(value, axis, [(source, source + steps) for source in range(leading, last)])


def elastic_blocks(stiffness, forward_table, adjoint_table, connect):
    count = connect.shape[1]
    block = math.gcd(count, 2048)
    grouped = connect.reshape(connect.shape[0], count // block, block).transpose(1, 0, 2)

    def one_block(piece):
        forward = jnp.take(forward_table, piece, axis=2)
        adjoint = jnp.take(adjoint_table, piece, axis=2)
        forward = forward.reshape(forward.shape[0], -1, forward.shape[3])
        adjoint = adjoint.reshape(adjoint.shape[0], -1, adjoint.shape[3])
        weighted = jnp.einsum("ab,tbe->tae", stiffness, forward, precision=lax.Precision.HIGHEST)
        return jnp.sum(adjoint * weighted, axis=(0, 1))

    return lax.map(one_block, grouped).reshape(-1)


def face_terms(press_a, press_b, adj_a, adj_b, perm_a, perm_b):
    product = jnp.sum((press_a - press_b) * (adj_a - adj_b), axis=0)
    denominator = (perm_a + perm_b) * (perm_a + perm_b)
    common = 2.0 * perm_a * perm_b * product / denominator
    return (common * perm_b, common * perm_a)


def on_device(
    displacement,
    adjoint_disp,
    pressure,
    adjoint_pressure,
    youngs,
    permeability,
    stiffness,
    send_nodes,
    send_cells,
    elem_nodes,
    inner_faces,
    cross_faces,
):
    step_count = displacement.shape[0]
    cell_count = youngs.shape[0]
    slot_count = len(OFFSETS)
    ghost_rows = send_cells.shape[1]
    received = []
    for slot_id in range(slot_count):
        node_rows = send_nodes[slot_id]
        cell_rows = send_cells[slot_id]
        out_forward = displacement[:, :, node_rows]
        out_adjoint = adjoint_disp[:, :, node_rows]
        out_cells = jnp.concatenate(
            [
                pressure[:, cell_rows],
                adjoint_pressure[:, cell_rows],
                permeability[cell_rows][None, :],
            ],
            axis=0,
        )
        arrived = shifted((out_forward, out_adjoint, out_cells), "dom", -OFFSETS[slot_id])
        received.append(arrived)
    forward_table = jnp.concatenate([displacement] + [piece[0] for piece in received], axis=2)
    adjoint_table = jnp.concatenate([adjoint_disp] + [piece[1] for piece in received], axis=2)
    ghost_cells = jnp.concatenate([piece[2] for piece in received], axis=1)
    strain = elastic_blocks(stiffness, forward_table, adjoint_table, elem_nodes)
    grad_youngs = -youngs * strain
    face_a = inner_faces[0]
    face_b = inner_faces[1]
    term_a, term_b = face_terms(
        pressure[:, face_a],
        pressure[:, face_b],
        adjoint_pressure[:, face_a],
        adjoint_pressure[:, face_b],
        permeability[face_a],
        permeability[face_b],
    )
    gradient = jnp.zeros((cell_count,), jnp.float32).at[face_a].add(term_a).at[face_b].add(term_b)
    own_cell = cross_faces[0]
    ghost_slot = cross_faces[1]
    ghost_press = ghost_cells[:step_count]
    ghost_adjpress = ghost_cells[step_count : 2 * step_count]
    ghost_perm = ghost_cells[2 * step_count]
    shared_a, shared_b = face_terms(
        pressure[:, own_cell],
        ghost_press[:, ghost_slot],
        adjoint_pressure[:, own_cell],
        ghost_adjpress[:, ghost_slot],
        permeability[own_cell],
        ghost_perm[ghost_slot],
    )
    gradient = gradient.at[own_cell].add(shared_a)
    returned = (
        jnp.zeros((slot_count * ghost_rows,), jnp.float32)
        .at[ghost_slot]
        .add(shared_b)
        .reshape(slot_count, ghost_rows)
    )
    for slot_id in range(slot_count):
        coming_back = shifted(returned[slot_id], "dom", OFFSETS[slot_id])
        gradient = gradient.at[send_cells[slot_id]].add(coming_back)
    return (grad_youngs, gradient)


def solution(mesh):
    in_specs = (
        P(None, None, "dom"),
        P(None, None, "dom"),
        P(None, "dom"),
        P(None, "dom"),
        P("dom"),
        P("dom"),
        P(),
        P(None, "dom"),
        P(None, "dom"),
        P(None, "dom"),
        P(None, "dom"),
        P(None, "dom"),
    )
    out_specs = (P("dom"), P("dom"))
    return jax.shard_map(
        on_device, mesh=mesh, in_specs=in_specs, out_specs=out_specs, check_vma=False
    )
```

profile of v0, /device:TPU:24, one launch (start us, length us, event | category | flops | bytes accessed | tf_op | source)
XLA Modules:
  0.0 859.4 jit_solution(17514860394995305429)
XLA Ops:
  0.7 4.2 copy.190
  10.1 9.6 %collective-permute-start.8 = (f32[8,3,128]{0,1,2:T(4,128)}, f32[8,3,128]{0,1,2:T(4,128)S(1)}, u32[]{:S(2)}, u32[]{:S(2)}) collective-permute-start(f32[8,3,128]{0,1,2:T(4,128)} %bitcast.27), channel_id=1, source_target_pairs={{1,0},{2,1},{3,2},{4,3},{5,4},{6,5},{7,6},{8,7},{9,8},{10,9},{11,1... | collective-permute-start | bytes 36872 | tf_op jit(solution)/shard_map/ppermute | solution.py:14
  43.1 3.9 constant_dynamic-update-slice_fusion.17
  47.2 34.3 %gather_fusion.16 = f32[6144]{0:T(1024)S(1)} fusion(f32[2048]{0:T(1024)S(1)} %copy-done.1, s32[6144]{0:T(1024)S(1)} %get-tuple-element.64), kind=kCustom, calls=%fused_computation.18 | custom fusion | bytes 73728 | tf_op jit(solution)/shard_map/gather | solution.py:86
  81.5 20.9 %gather_fusion.20 = f32[6144,8]{1,0:T(8,128)} fusion(f32[8,2048]{0,1:T(8,128)S(1)} %copy.194, s32[6144]{0:T(1024)S(1)} %get-tuple-element.64), kind=kCustom, calls=%fused_computation.22 | custom fusion | bytes 417792 | tf_op jit(solution)/shard_map/gather | solution.py:84
  102.4 34.3 %gather_fusion.17 = f32[6144]{0:T(1024)S(1)} fusion(f32[2048]{0:T(1024)S(1)} %copy-done.1, s32[6144]{0:T(1024)S(1)} %get-tuple-element.63), kind=kCustom, calls=%fused_computation.19 | custom fusion | bytes 73728 | tf_op jit(solution)/shard_map/gather | solution.py:87
  136.7 20.9 %gather_fusion.21 = f32[6144,8]{1,0:T(8,128)} fusion(f32[8,2048]{0,1:T(8,128)S(1)} %copy.194, s32[6144]{0:T(1024)S(1)} %get-tuple-element.63), kind=kCustom, calls=%fused_computation.23 | custom fusion | bytes 417792 | tf_op jit(solution)/shard_map/gather | solution.py:85
  157.5 20.9 %gather_fusion.18 = f32[6144,8]{1,0:T(8,128)} fusion(f32[8,2048]{0,1:T(8,128)S(1)} %copy.192, s32[6144]{0:T(1024)S(1)} %get-tuple-element.64), kind=kCustom, calls=%fused_computation.20 | custom fusion | bytes 417792 | tf_op jit(solution)/shard_map/gather | solution.py:82
  178.4 20.9 %gather_fusion.19 = f32[6144,8]{1,0:T(8,128)} fusion(f32[8,2048]{0,1:T(8,128)S(1)} %copy.192, s32[6144]{0:T(1024)S(1)} %get-tuple-element.63), kind=kCustom, calls=%fused_computation.21 | custom fusion | bytes 417792 | tf_op jit(solution)/shard_map/gather | solution.py:83
  218.9 5.5 multiply_reduce_fusion
  278.5 6.2 gather_fusion.22
  290.3 32.8 %scatter_custom_fusion = f32[2048]{0:T(1024)S(1)} fusion(s32[6144]{0:T(1024)S(1)} %bitcast.151, f32[6144]{0:T(1024)S(1)} %get-tuple-element.24, f32[]{:T(128)} %constant.15.clone.1), kind=kCustom, calls=%fused_computation.137 | custom fusion | flops 6144 | bytes 8196 | tf_op jit(solution)/shard_map/scatter-add | solution.py:89
  333.7 6.2 collective-permute-start.23
  340.0 6.2 collective-permute-done.23
  346.4 4.5 gather_fusion.47
  357.0 7.6 scatter_custom_fusion.3
  367.9 33.7 %scatter_fusion = f32[2048]{0:T(1024)S(1)} fusion(f32[2048]{0:T(1024)S(1)} %scatter_custom_fusion, s32[6144]{0:T(1024)S(1)} %bitcast.149, f32[6144]{0:T(1024)S(1)} %get-tuple-element.17), kind=kCustom, calls=%fused_computation.55 | custom fusion | flops 6144 | bytes 98304 | tf_op jit(solution)/shard_map/scatter-add | solution.py:89
  401.6 10.7 %collective-permute-start.25 = (f32[128]{0:T(128)S(1)}, f32[128]{0:T(128)S(1)}, u32[]{:S(2)}, u32[]{:S(2)}) collective-permute-start(f32[128]{0:T(128)S(1)} %get-tuple-element.37), channel_id=1, source_target_pairs={{1,0},{2,1},{3,2},{4,3},{5,4},{6,5},{7,6},{8,7},{9,8},{10,9},{11,1... | collective-permute-start | bytes 1544 | tf_op jit(solution)/shard_map/ppermute | solution.py:14
  414.3 8.1 collective-permute-start.27
  422.5 6.1 scatter_fusion.1
  432.0 9.0 %collective-permute-start.29 = (f32[128]{0:T(128)S(1)}, f32[128]{0:T(128)S(1)}, u32[]{:S(2)}, u32[]{:S(2)}) collective-permute-start(f32[128]{0:T(128)S(1)} %get-tuple-element.33), channel_id=1, source_target_pairs={{4,0},{5,1},{6,2},{7,3},{8,4},{9,5},{10,6},{11,7},{12,8},{13,9},{1... | collective-permute-start | bytes 1544 | tf_op jit(solution)/shard_map/ppermute | solution.py:14
  445.5 10.8 %collective-permute-start.31 = (f32[128]{0:T(128)S(1)}, f32[128]{0:T(128)S(1)}, u32[]{:S(2)}, u32[]{:S(2)}) collective-permute-start(f32[128]{0:T(128)S(1)} %get-tuple-element.31), channel_id=1, source_target_pairs={{8,0},{9,1},{10,2},{11,3},{12,4},{13,5},{14,6},{15,7},{16,8},{17,9... | collective-permute-start | bytes 1544 | tf_op jit(solution)/shard_map/ppermute | solution.py:14
  472.5 4.8 collective-permute-start.13
  480.8 7.8 collective-permute-start.15
  489.4 17.6 %collective-permute-start = (f32[8,3,128]{0,1,2:T(4,128)}, f32[8,3,128]{0,1,2:T(4,128)S(1)}, u32[]{:S(2)}, u32[]{:S(2)}) collective-permute-start(f32[8,3,128]{0,1,2:T(4,128)} %bitcast.2), channel_id=1, source_target_pairs={{1,0},{2,1},{3,2},{4,3},{5,4},{6,5},{7,6},{8,7},{9,8},{10,9},{11,1... | collective-permute-start | bytes 36872 | tf_op jit(solution)/shard_map/ppermute | solution.py:14
  521.7 121.3 %gather_fusion.53 = f32[16384,8,3]{1,2,0:T(4,128)} fusion(f32[8,3,3072]{0,1,2:T(4,128)} %constant_dynamic-update-slice_fusion.9, s32[16384]{0:T(1024)S(1)} %broadcast_clamp_fusion), kind=kCustom, calls=%fused_computation.1.clone | custom fusion | bytes 3211264 | tf_op jit(solution)/shard_map/while/body/eval_jaxpr/jit(_take)/gather | solution.py:23
  643.0 25.4 %select_bitcast_fusion = f32[8,3,8,2048]{0,1,3,2:T(4,128)} fusion(f32[8,2048,8,3]{2,3,1,0:T(4,128)} %bitcast.145, pred[8,2048]{1,0:T(8,128)(4,1)S(1)} %compare_and_fusion), kind=kLoop, calls=%fused_computation.66 | loop fusion | flops 393216 | bytes 3162112 | tf_op jit(solution)/shard_map/while/body/eval_jaxpr/jit(_take)/select_n | solution.py:23
  676.3 6.9 collective-permute-start.7
  685.5 11.8 %collective-permute-done.5 = f32[8,3,128]{0,1,2:T(4,128)S(1)} collective-permute-done((f32[8,3,128]{0,1,2:T(4,128)S(1)}, f32[8,3,128]{0,1,2:T(4,128)S(1)}, u32[]{:S(2)}, u32[]{:S(2)}) %collective-permute-start.5) | collective-permute-done | bytes 12320 | tf_op jit(solution)/shard_map/ppermute | solution.py:14
  698.8 18.0 %copy.191 = f32[8,3,8,2048]{3,2,1,0:T(8,128)S(1)} copy(f32[8,3,8,2048]{0,1,3,2:T(4,128)} %select_bitcast_fusion) | data formatting | bytes 3145728 | tf_op jit(solution)/shard_map/while/body/eval_jaxpr/jit(_take)/select_n | solution.py:23
  717.6 121.6 %gather_fusion.52 = f32[16384,8,3]{1,2,0:T(4,128)} fusion(f32[8,3,3072]{0,1,2:T(4,128)} %constant_dynamic-update-slice_fusion, s32[16384]{0:T(1024)S(1)} %broadcast_clamp_fusion), kind=kCustom, calls=%fused_computation.clone | custom fusion | bytes 3211264 | tf_op jit(solution)/shard_map/while/body/eval_jaxpr/jit(_take)/gather | solution.py:24
  839.1 18.0 %copy.181 = f32[8,2048,8,3]{1,0,3,2:T(8,128)S(1)} copy(f32[8,2048,8,3]{2,3,1,0:T(4,128)} %bitcast.146) | data formatting | bytes 3145728 | tf_op jit(solution)/shard_map/while/body/eval_jaxpr/jit(_take)/gather | solution.py:24
  (260 shorter events, 186.7 us)
Async XLA Ops:
  10.1 462.5 %collective-permute-start.8 = (f32[8,3,128]{0,1,2:T(4,128)}, f32[8,3,128]{0,1,2:T(4,128)S(1)}, u32[]{:S(2)}, u32[]{:S(2)}) collective-permute-start(f32[8,3,128]{0,1,2:T(4,128)} %bitcast.27), channel_id=1, source_target_pairs={{1,0},{2,1},{3,2},{4,3},{5,4},{6,5},{7,6},{8,7},{9,8},{10,9},{11,1... | collective-permute-start | bytes 36872 | tf_op jit(solution)/shard_map/ppermute | solution.py:14
  24.8 298.3 %collective-permute-start.16 = (f32[17,128]{1,0:T(8,128)S(1)}, f32[17,128]{1,0:T(8,128)S(1)}, u32[]{:S(2)}, u32[]{:S(2)}) collective-permute-start(f32[17,128]{1,0:T(8,128)S(1)} %pad_maximum_fusion), channel_id=1, source_target_pairs={{1,0},{2,1},{3,2},{4,3},{5,4},{6,5},{7,6},{8,7},{9,8},{10,9},{11,1... | collective-permute-start | bytes 26120 | tf_op jit(solution)/shard_map/ppermute | solution.py:14
  29.9 296.6 %collective-permute-start.17 = (f32[17,128]{1,0:T(8,128)S(1)}, f32[17,128]{1,0:T(8,128)S(1)}, u32[]{:S(2)}, u32[]{:S(2)}) collective-permute-start(f32[17,128]{1,0:T(8,128)S(1)} %pad_maximum_fusion.1), channel_id=1, source_target_pairs={{0,1},{1,2},{2,3},{3,4},{4,5},{5,6},{6,7},{7,8},{8,9},{9,10},{10,1... | collective-permute-start | bytes 26120 | tf_op jit(solution)/shard_map/ppermute | solution.py:14
  34.5 295.4 %collective-permute-start.18 = (f32[17,128]{1,0:T(8,128)S(1)}, f32[17,128]{1,0:T(8,128)S(1)}, u32[]{:S(2)}, u32[]{:S(2)}) collective-permute-start(f32[17,128]{1,0:T(8,128)S(1)} %pad_maximum_fusion.2), channel_id=1, source_target_pairs={{2,0},{3,1},{4,2},{5,3},{6,4},{7,5},{8,6},{9,7},{10,8},{11,9},{12,... | collective-permute-start | bytes 26120 | tf_op jit(solution)/shard_map/ppermute | solution.py:14
  40.0 293.7 %collective-permute-start.19 = (f32[17,128]{1,0:T(8,128)S(1)}, f32[17,128]{1,0:T(8,128)S(1)}, u32[]{:S(2)}, u32[]{:S(2)}) collective-permute-start(f32[17,128]{1,0:T(8,128)S(1)} %pad_maximum_fusion.3), channel_id=1, source_target_pairs={{0,2},{1,3},{2,4},{3,5},{4,6},{5,7},{6,8},{7,9},{8,10},{9,11},{10,... | collective-permute-start | bytes 26120 | tf_op jit(solution)/shard_map/ppermute | solution.py:14
  323.1 16.8 %collective-permute-start.20 = (f32[17,128]{1,0:T(8,128)S(1)}, f32[17,128]{1,0:T(8,128)S(1)}, u32[]{:S(2)}, u32[]{:S(2)}) collective-permute-start(f32[17,128]{1,0:T(8,128)S(1)} %pad_maximum_fusion.4), channel_id=1, source_target_pairs={{4,0},{5,1},{6,2},{7,3},{8,4},{9,5},{10,6},{11,7},{12,8},{13,9},{1... | collective-permute-start | bytes 26120 | tf_op jit(solution)/shard_map/ppermute | solution.py:14
  326.6 13.4 %collective-permute-start.21 = (f32[17,128]{1,0:T(8,128)S(1)}, f32[17,128]{1,0:T(8,128)S(1)}, u32[]{:S(2)}, u32[]{:S(2)}) collective-permute-start(f32[17,128]{1,0:T(8,128)S(1)} %pad_maximum_fusion.5), channel_id=1, source_target_pairs={{0,4},{1,5},{2,6},{3,7},{4,8},{5,9},{6,10},{7,11},{8,12},{9,13},{1... | collective-permute-start | bytes 26120 | tf_op jit(solution)/shard_map/ppermute | solution.py:14
  329.9 10.1 %collective-permute-start.22 = (f32[17,128]{1,0:T(8,128)S(1)}, f32[17,128]{1,0:T(8,128)S(1)}, u32[]{:S(2)}, u32[]{:S(2)}) collective-permute-start(f32[17,128]{1,0:T(8,128)S(1)} %pad_maximum_fusion.6), channel_id=1, source_target_pairs={{8,0},{9,1},{10,2},{11,3},{12,4},{13,5},{14,6},{15,7},{16,8},{17,9... | collective-permute-start | bytes 26120 | tf_op jit(solution)/shard_map/ppermute | solution.py:14
  333.7 12.5 %collective-permute-start.23 = (f32[17,128]{1,0:T(8,128)S(1)}, f32[17,128]{1,0:T(8,128)S(1)}, u32[]{:S(2)}, u32[]{:S(2)}) collective-permute-start(f32[17,128]{1,0:T(8,128)S(1)} %pad_maximum_fusion.7), channel_id=1, source_target_pairs={{0,8},{1,9},{2,10},{3,11},{4,12},{5,13},{6,14},{7,15},{8,16},{9,17... | collective-permute-start | bytes 26120 | tf_op jit(solution)/shard_map/ppermute | solution.py:14
  364.7 64.0 %collective-permute-start.24 = (f32[128]{0:T(128)S(1)}, f32[128]{0:T(128)S(1)}, u32[]{:S(2)}, u32[]{:S(2)}) collective-permute-start(f32[128]{0:T(128)S(1)} %get-tuple-element.38), channel_id=1, source_target_pairs={{0,1},{1,2},{2,3},{3,4},{4,5},{5,6},{6,7},{7,8},{8,9},{9,10},{10,1... | collective-permute-start | bytes 1544 | tf_op jit(solution)/shard_map/ppermute | solution.py:14
  401.6 30.4 %collective-permute-start.25 = (f32[128]{0:T(128)S(1)}, f32[128]{0:T(128)S(1)}, u32[]{:S(2)}, u32[]{:S(2)}) collective-permute-start(f32[128]{0:T(128)S(1)} %get-tuple-element.37), channel_id=1, source_target_pairs={{1,0},{2,1},{3,2},{4,3},{5,4},{6,5},{7,6},{8,7},{9,8},{10,9},{11,1... | collective-permute-start | bytes 1544 | tf_op jit(solution)/shard_map/ppermute | solution.py:14
  412.4 30.0 %collective-permute-start.26 = (f32[128]{0:T(128)S(1)}, f32[128]{0:T(128)S(1)}, u32[]{:S(2)}, u32[]{:S(2)}) collective-permute-start(f32[128]{0:T(128)S(1)} %get-tuple-element.36), channel_id=1, source_target_pairs={{0,2},{1,3},{2,4},{3,5},{4,6},{5,7},{6,8},{7,9},{8,10},{9,11},{10,... | collective-permute-start | bytes 1544 | tf_op jit(solution)/shard_map/ppermute | solution.py:14
  414.3 31.2 %collective-permute-start.27 = (f32[128]{0:T(128)S(1)}, f32[128]{0:T(128)S(1)}, u32[]{:S(2)}, u32[]{:S(2)}) collective-permute-start(f32[128]{0:T(128)S(1)} %get-tuple-element.35), channel_id=1, source_target_pairs={{2,0},{3,1},{4,2},{5,3},{6,4},{7,5},{8,6},{9,7},{10,8},{11,9},{12,... | collective-permute-start | bytes 1544 | tf_op jit(solution)/shard_map/ppermute | solution.py:14
  428.7 29.0 %collective-permute-start.28 = (f32[128]{0:T(128)S(1)}, f32[128]{0:T(128)S(1)}, u32[]{:S(2)}, u32[]{:S(2)}) collective-permute-start(f32[128]{0:T(128)S(1)} %get-tuple-element.34), channel_id=1, source_target_pairs={{0,4},{1,5},{2,6},{3,7},{4,8},{5,9},{6,10},{7,11},{8,12},{9,13},{1... | collective-permute-start | bytes 1544 | tf_op jit(solution)/shard_map/ppermute | solution.py:14
  432.0 28.8 %collective-permute-start.29 = (f32[128]{0:T(128)S(1)}, f32[128]{0:T(128)S(1)}, u32[]{:S(2)}, u32[]{:S(2)}) collective-permute-start(f32[128]{0:T(128)S(1)} %get-tuple-element.33), channel_id=1, source_target_pairs={{4,0},{5,1},{6,2},{7,3},{8,4},{9,5},{10,6},{11,7},{12,8},{13,9},{1... | collective-permute-start | bytes 1544 | tf_op jit(solution)/shard_map/ppermute | solution.py:14
  442.3 21.8 %collective-permute-start.30 = (f32[128]{0:T(128)S(1)}, f32[128]{0:T(128)S(1)}, u32[]{:S(2)}, u32[]{:S(2)}) collective-permute-start(f32[128]{0:T(128)S(1)} %get-tuple-element.32), channel_id=1, source_target_pairs={{0,8},{1,9},{2,10},{3,11},{4,12},{5,13},{6,14},{7,15},{8,16},{9,17... | collective-permute-start | bytes 1544 | tf_op jit(solution)/shard_map/ppermute | solution.py:14
  445.5 23.8 %collective-permute-start.31 = (f32[128]{0:T(128)S(1)}, f32[128]{0:T(128)S(1)}, u32[]{:S(2)}, u32[]{:S(2)}) collective-permute-start(f32[128]{0:T(128)S(1)} %get-tuple-element.31), channel_id=1, source_target_pairs={{8,0},{9,1},{10,2},{11,3},{12,4},{13,5},{14,6},{15,7},{16,8},{17,9... | collective-permute-start | bytes 1544 | tf_op jit(solution)/shard_map/ppermute | solution.py:14
  457.7 20.5 %collective-permute-start.9 = (f32[8,3,128]{0,1,2:T(4,128)S(1)}, f32[8,3,128]{0,1,2:T(4,128)S(1)}, u32[]{:S(2)}, u32[]{:S(2)}) collective-permute-start(f32[8,3,128]{0,1,2:T(4,128)S(1)} %bitcast.187), channel_id=1, source_target_pairs={{0,1},{1,2},{2,3},{3,4},{4,5},{5,6},{6,7},{7,8},{8,9},{9,10},{10,1... | collective-permute-start | bytes 36872 | tf_op jit(solution)/shard_map/ppermute | solution.py:14
  460.9 19.9 %collective-permute-start.10 = (f32[8,3,128]{0,1,2:T(4,128)S(1)}, f32[8,3,128]{0,1,2:T(4,128)S(1)}, u32[]{:S(2)}, u32[]{:S(2)}) collective-permute-start(f32[8,3,128]{0,1,2:T(4,128)S(1)} %bitcast.186), channel_id=1, source_target_pairs={{2,0},{3,1},{4,2},{5,3},{6,4},{7,5},{8,6},{9,7},{10,8},{11,9},{12,... | collective-permute-start | bytes 36872 | tf_op jit(solution)/shard_map/ppermute | solution.py:14
  464.1 25.3 %collective-permute-start.11 = (f32[8,3,128]{0,1,2:T(4,128)}, f32[8,3,128]{0,1,2:T(4,128)S(1)}, u32[]{:S(2)}, u32[]{:S(2)}) collective-permute-start(f32[8,3,128]{0,1,2:T(4,128)} %bitcast.30), channel_id=1, source_target_pairs={{0,2},{1,3},{2,4},{3,5},{4,6},{5,7},{6,8},{7,9},{8,10},{9,11},{10,... | collective-permute-start | bytes 36872 | tf_op jit(solution)/shard_map/ppermute | solution.py:14
  469.3 38.5 %collective-permute-start.12 = (f32[8,3,128]{0,1,2:T(4,128)}, f32[8,3,128]{0,1,2:T(4,128)S(1)}, u32[]{:S(2)}, u32[]{:S(2)}) collective-permute-start(f32[8,3,128]{0,1,2:T(4,128)} %bitcast.31), channel_id=1, source_target_pairs={{4,0},{5,1},{6,2},{7,3},{8,4},{9,5},{10,6},{11,7},{12,8},{13,9},{1... | collective-permute-start | bytes 36872 | tf_op jit(solution)/shard_map/ppermute | solution.py:14
  472.5 38.0 %collective-permute-start.13 = (f32[8,3,128]{0,1,2:T(4,128)}, f32[8,3,128]{0,1,2:T(4,128)S(1)}, u32[]{:S(2)}, u32[]{:S(2)}) collective-permute-start(f32[8,3,128]{0,1,2:T(4,128)} %bitcast.32), channel_id=1, source_target_pairs={{0,4},{1,5},{2,6},{3,7},{4,8},{5,9},{6,10},{7,11},{8,12},{9,13},{1... | collective-permute-start | bytes 36872 | tf_op jit(solution)/shard_map/ppermute | solution.py:14
  478.1 35.4 %collective-permute-start.14 = (f32[8,3,128]{0,1,2:T(4,128)}, f32[8,3,128]{0,1,2:T(4,128)S(1)}, u32[]{:S(2)}, u32[]{:S(2)}) collective-permute-start(f32[8,3,128]{0,1,2:T(4,128)} %bitcast.33), channel_id=1, source_target_pairs={{8,0},{9,1},{10,2},{11,3},{12,4},{13,5},{14,6},{15,7},{16,8},{17,9... | collective-permute-start | bytes 36872 | tf_op jit(solution)/shard_map/ppermute | solution.py:14
  480.8 37.0 %collective-permute-start.15 = (f32[8,3,128]{0,1,2:T(4,128)S(1)}, f32[8,3,128]{0,1,2:T(4,128)S(1)}, u32[]{:S(2)}, u32[]{:S(2)}) collective-permute-start(f32[8,3,128]{0,1,2:T(4,128)S(1)} %bitcast.185), channel_id=1, source_target_pairs={{0,8},{1,9},{2,10},{3,11},{4,12},{5,13},{6,14},{7,15},{8,16},{9,17... | collective-permute-start | bytes 36872 | tf_op jit(solution)/shard_map/ppermute | solution.py:14
  489.4 179.0 %collective-permute-start = (f32[8,3,128]{0,1,2:T(4,128)}, f32[8,3,128]{0,1,2:T(4,128)S(1)}, u32[]{:S(2)}, u32[]{:S(2)}) collective-permute-start(f32[8,3,128]{0,1,2:T(4,128)} %bitcast.2), channel_id=1, source_target_pairs={{1,0},{2,1},{3,2},{4,3},{5,4},{6,5},{7,6},{8,7},{9,8},{10,9},{11,1... | collective-permute-start | bytes 36872 | tf_op jit(solution)/shard_map/ppermute | solution.py:14
  507.8 164.9 %collective-permute-start.1 = (f32[8,3,128]{0,1,2:T(4,128)}, f32[8,3,128]{0,1,2:T(4,128)S(1)}, u32[]{:S(2)}, u32[]{:S(2)}) collective-permute-start(f32[8,3,128]{0,1,2:T(4,128)} %bitcast.5), channel_id=1, source_target_pairs={{0,1},{1,2},{2,3},{3,4},{4,5},{5,6},{6,7},{7,8},{8,9},{9,10},{10,1... | collective-permute-start | bytes 36872 | tf_op jit(solution)/shard_map/ppermute | solution.py:14
  510.5 165.8 %collective-permute-start.2 = (f32[8,3,128]{0,1,2:T(4,128)S(1)}, f32[8,3,128]{0,1,2:T(4,128)S(1)}, u32[]{:S(2)}, u32[]{:S(2)}) collective-permute-start(f32[8,3,128]{0,1,2:T(4,128)S(1)} %bitcast.184), channel_id=1, source_target_pairs={{2,0},{3,1},{4,2},{5,3},{6,4},{7,5},{8,6},{9,7},{10,8},{11,9},{12,... | collective-permute-start | bytes 36872 | tf_op jit(solution)/shard_map/ppermute | solution.py:14
  513.5 170.5 %collective-permute-start.3 = (f32[8,3,128]{0,1,2:T(4,128)}, f32[8,3,128]{0,1,2:T(4,128)S(1)}, u32[]{:S(2)}, u32[]{:S(2)}) collective-permute-start(f32[8,3,128]{0,1,2:T(4,128)} %bitcast.11), channel_id=1, source_target_pairs={{0,2},{1,3},{2,4},{3,5},{4,6},{5,7},{6,8},{7,9},{8,10},{9,11},{10,... | collective-permute-start | bytes 36872 | tf_op jit(solution)/shard_map/ppermute | solution.py:14
  517.8 166.9 %collective-permute-start.4 = (f32[8,3,128]{0,1,2:T(4,128)S(1)}, f32[8,3,128]{0,1,2:T(4,128)S(1)}, u32[]{:S(2)}, u32[]{:S(2)}) collective-permute-start(f32[8,3,128]{0,1,2:T(4,128)S(1)} %bitcast.183), channel_id=1, source_target_pairs={{4,0},{5,1},{6,2},{7,3},{8,4},{9,5},{10,6},{11,7},{12,8},{13,9},{1... | collective-permute-start | bytes 36872 | tf_op jit(solution)/shard_map/ppermute | solution.py:14
  668.4 28.9 %collective-permute-start.5 = (f32[8,3,128]{0,1,2:T(4,128)S(1)}, f32[8,3,128]{0,1,2:T(4,128)S(1)}, u32[]{:S(2)}, u32[]{:S(2)}) collective-permute-start(f32[8,3,128]{0,1,2:T(4,128)S(1)} %bitcast.182), channel_id=1, source_target_pairs={{0,4},{1,5},{2,6},{3,7},{4,8},{5,9},{6,10},{7,11},{8,12},{9,13},{1... | collective-permute-start | bytes 36872 | tf_op jit(solution)/shard_map/ppermute | solution.py:14
  672.7 25.3 %collective-permute-start.6 = (f32[8,3,128]{0,1,2:T(4,128)S(1)}, f32[8,3,128]{0,1,2:T(4,128)S(1)}, u32[]{:S(2)}, u32[]{:S(2)}) collective-permute-start(f32[8,3,128]{0,1,2:T(4,128)S(1)} %bitcast.181), channel_id=1, source_target_pairs={{8,0},{9,1},{10,2},{11,3},{12,4},{13,5},{14,6},{15,7},{16,8},{17,9... | collective-permute-start | bytes 36872 | tf_op jit(solution)/shard_map/ppermute | solution.py:14
  676.3 40.5 %collective-permute-start.7 = (f32[8,3,128]{0,1,2:T(4,128)S(1)}, f32[8,3,128]{0,1,2:T(4,128)S(1)}, u32[]{:S(2)}, u32[]{:S(2)}) collective-permute-start(f32[8,3,128]{0,1,2:T(4,128)S(1)} %bitcast.180), channel_id=1, source_target_pairs={{0,8},{1,9},{2,10},{3,11},{4,12},{5,13},{6,14},{7,15},{8,16},{9,17... | collective-permute-start | bytes 36872 | tf_op jit(solution)/shard_map/ppermute | solution.py:14
  (38 other events, 2733.3 us)
where the time goes:
time: 875 us; the launch traced here: 859 us
  local copies, waits for them, and re-layouts  563 us (64%)
  starting transfers between devices  151 us (17%)
  other arithmetic  124 us (14%)
  waiting for transfers between devices  18.1 us (2%)
    ppermute x32, starting transfers between devices, shifted(): lax.ppermute(value, axis, [(source, source + steps) for source in range(l...  151 us
    gather x2, local copies, waits for them, and re-layouts, one_block(): adjoint = jnp.take(adjoint_table, piece, axis=2)  140 us
    gather x1, local copies, waits for them, and re-layouts, one_block(): forward = jnp.take(forward_table, piece, axis=2)  121 us
    scatter-add x2, other arithmetic, on_device(): jnp.zeros((cell_count,), jnp.float32).at[face_a].add(term_a).at[face_b]  66.4 us
    gather x1, local copies, waits for them, and re-layouts, on_device(): permeability[face_a]  34.3 us
    gather x1, local copies, waits for them, and re-layouts, on_device(): permeability[face_b]  34.3 us
    gather x8, local copies, waits for them, and re-layouts, on_device(): out_forward = displacement[:, :, node_rows]  29.1 us
    gather x8, local copies, waits for them, and re-layouts, on_device(): out_adjoint = adjoint_disp[:, :, node_rows]  28.4 us
  transfers between devices with their start and end apart: 32, of which 2 were waited for; matrix products, arithmetic and copies ran while one was open for 62% of the time, Pallas kernels for 0%

commit v1 on v0

v1 whole, which is shorter than its diff:
```python
import functools

import jax
import jax.numpy as jnp
from jax import lax
from jax.experimental import pallas as pl
from jax.experimental.pallas import tpu as pltpu
from jax.sharding import PartitionSpec as P

OFFSETS = (1, -1, 2, -2, 4, -4, 8, -8)
MESH = pl.DeviceIdType.MESH
F32 = jnp.float32
BF16 = jnp.bfloat16
LANES = 128
STEPS = 8
OWN = 16
NB = 8
CELL_ROWS = 24
NODE_ROWS = 48
CELL_BLOCKS = 6
INNER_BLOCKS = 12
ALL_BLOCKS = 16


def take(source, lanes):
    return jnp.take_along_axis(source, lanes, axis=1, mode="promise_in_bounds")


def pick(values, bits):
    if len(values) == 1:
        return values[0]()
    half = len(values) // 2
    top = bits[half.bit_length() - 1]
    low = pick(values[:half], bits)
    high = pick(values[half:], bits)
    return jnp.where(top, high, low)


def spread(ref, row, column):
    return jnp.broadcast_to(ref[row : row + 1, column : column + LANES], (8, LANES))


def bit_masks(chunk, count):
    return [(chunk & (1 << bit)) != 0 for bit in range(count)]


def own_rows(ref, row, lanes, bits):
    return pick(
        [lambda h=h: take(spread(ref, row, h * LANES), lanes) for h in range(OWN)],
        bits,
    )


def own_perm(ref, lanes, bits):
    return pick([lambda h=h: take(spread(ref, h, 0), lanes) for h in range(OWN)], bits)


def ghost_rows(ref, row, pitch, lanes, bits):
    return pick(
        [lambda j=j: take(spread(ref, j * pitch + row, 0), lanes) for j in range(NB)],
        bits,
    )


def split(value):
    high = value.astype(BF16).astype(F32)
    return high, value - high


def contract_lanes(left, right):
    return lax.dot_general(
        left, right, (((1,), (1,)), ((), ())), preferred_element_type=F32
    )


def scatter_rows(index, value_ref, rows, index_row):
    chunk_iota = lax.broadcasted_iota(jnp.int32, (rows, LANES), 0)
    lane_iota = lax.broadcasted_iota(jnp.int32, (LANES, LANES), 0)
    left, right = [], []
    for s in range(8):
        where = index_row(s)
        value = jnp.broadcast_to(value_ref[s : s + 1, :], (rows, LANES))
        chunk = jnp.broadcast_to(where >> 7, (rows, LANES))
        left.append(jnp.where(chunk == chunk_iota, value, 0.0))
        lane = jnp.broadcast_to(where & 127, (LANES, LANES))
        right.append(jnp.where(lane == lane_iota, 1.0, 0.0).astype(BF16))
    wide = jnp.concatenate(left, axis=1)
    high, low = split(wide)
    both = jnp.concatenate([high, low], axis=0).astype(BF16)
    summed = contract_lanes(both, jnp.concatenate(right, axis=1))
    return summed[:rows] + summed[rows:]


def face_common(perm_a, perm_b, product):
    both = perm_a + perm_b
    return 2.0 * perm_a * perm_b * product / (both * both)


def kernel(
    count,
    disp_ref,
    adj_ref,
    press_ref,
    apress_ref,
    youngs_ref,
    perm_ref,
    stiff_ref,
    send_nodes_ref,
    send_cells_ref,
    elem_ref,
    inner_ref,
    cross_ref,
    gy_ref,
    gp_ref,
    cells_out,
    nodes_out,
    cells_in,
    nodes_in,
    back_out,
    back_in,
    term_a_ref,
    term_b_ref,
    cell_send,
    cell_recv,
    node_send,
    node_recv,
    back_send,
    back_recv,
):
    me = lax.axis_index("dom")

    def at(offset):
        return (lax.rem(me + (offset + count), count),)

    barrier = pltpu.get_barrier_semaphore()
    for offset in OFFSETS:
        pl.semaphore_signal(barrier, inc=1, device_id=at(offset), device_id_type=MESH)

    index = send_cells_ref[...]
    lanes, bits = index & 127, bit_masks(index >> 7, 4)
    for t in range(STEPS):
        cells_out[pl.ds(t, NB, stride=CELL_ROWS), :] = own_rows(press_ref, t, lanes, bits)
        cells_out[pl.ds(STEPS + t, NB, stride=CELL_ROWS), :] = own_rows(
            apress_ref, t, lanes, bits
        )
    for r in range(2 * STEPS, CELL_ROWS):
        if r == 2 * STEPS:
            permeability = own_perm(perm_ref, lanes, bits)
        cells_out[pl.ds(r, NB, stride=CELL_ROWS), :] = permeability
    index = send_nodes_ref[...]
    lanes, bits = index & 127, bit_masks(index >> 7, 4)
    for r in range(24):
        nodes_out[pl.ds(r, NB, stride=NODE_ROWS), :] = own_rows(disp_ref, r, lanes, bits)
        nodes_out[pl.ds(24 + r, NB, stride=NODE_ROWS), :] = own_rows(
            adj_ref, r, lanes, bits
        )

    pl.semaphore_wait(barrier, NB)

    def cell_copy(j):
        return pltpu.make_async_remote_copy(
            src_ref=cells_out.at[pl.ds(j * CELL_ROWS, CELL_ROWS)],
            dst_ref=cells_in.at[pl.ds(j * CELL_ROWS, CELL_ROWS)],
            send_sem=cell_send.at[j],
            recv_sem=cell_recv.at[j],
            device_id=at(-OFFSETS[j]),
            device_id_type=MESH,
        )

    def node_copy(j):
        return pltpu.make_async_remote_copy(
            src_ref=nodes_out.at[pl.ds(j * NODE_ROWS, NODE_ROWS)],
            dst_ref=nodes_in.at[pl.ds(j * NODE_ROWS, NODE_ROWS)],
            send_sem=node_send.at[j],
            recv_sem=node_recv.at[j],
            device_id=at(-OFFSETS[j]),
            device_id_type=MESH,
        )

    def back_copy(j):
        return pltpu.make_async_remote_copy(
            src_ref=back_out,
            dst_ref=back_in.at[pl.ds(8 * j, 8)],
            send_sem=back_send.at[j],
            recv_sem=back_recv.at[j],
            device_id=at(OFFSETS[j]),
            device_id_type=MESH,
        )

    for j in range(NB):
        cell_copy(j).start()
    for j in range(NB):
        node_copy(j).start()

    def inner_faces(block, gradient):
        base = pl.multiple_of(block * 16, 16)
        ends = []
        for side in range(2):
            index = inner_ref[pl.ds(base + side, 8, stride=2), :]
            lanes, bits = index & 127, bit_masks(index >> 7, 4)
            ends.append(
                (
                    [own_rows(press_ref, t, lanes, bits) for t in range(STEPS)],
                    [own_rows(apress_ref, t, lanes, bits) for t in range(STEPS)],
                    own_perm(perm_ref, lanes, bits),
                )
            )
        (pa, qa, ka), (pb, qb, kb) = ends
        product = sum((pa[t] - pb[t]) * (qa[t] - qb[t]) for t in range(STEPS))
        common = face_common(ka, kb, product)
        term_a_ref[...] = common * kb
        term_b_ref[...] = common * ka
        for side, term_ref in enumerate((term_a_ref, term_b_ref)):
            gradient = gradient + scatter_rows(
                None,
                term_ref,
                OWN,
                lambda s: inner_ref[pl.ds(base + 2 * s + side, 1), :],
            )
        return gradient

    gradient = lax.fori_loop(0, CELL_BLOCKS, inner_faces, jnp.zeros((OWN, LANES), F32))

    stiff_high, stiff_low = split(stiff_ref[...])
    stiff = jnp.concatenate([stiff_high, stiff_low, stiff_high], axis=1).astype(BF16)

    def elements(block, ghosts):
        column = pl.multiple_of(block * LANES, LANES)
        index = elem_ref[:, pl.ds(column, LANES)]
        lanes, chunk = index & 127, index >> 7
        bits = bit_masks(chunk, 4)
        outside = chunk >= OWN

        def corner_rows(ref, row, ghost_row):
            value = own_rows(ref, row, lanes, bits)
            if ghosts:
                value = jnp.where(
                    outside, ghost_rows(nodes_in, ghost_row, NODE_ROWS, lanes, bits), value
                )
            return value

        total = jnp.zeros((8, LANES), F32)
        for t in range(STEPS):
            forward = jnp.concatenate(
                [corner_rows(disp_ref, 8 * c + t, 8 * c + t) for c in range(3)], axis=0
            )
            adjoint = [corner_rows(adj_ref, 8 * c + t, 24 + 8 * c + t) for c in range(3)]
            high, low = split(forward)
            stacked = jnp.concatenate([high, high, low], axis=0).astype(BF16)
            weighted = jnp.dot(stiff, stacked, preferred_element_type=F32)
            for c in range(3):
                total = total + adjoint[c] * weighted[8 * c : 8 * c + 8]
        strain = jnp.sum(total, axis=0, keepdims=True)
        gy_ref[pl.ds(block, 1), :] = -youngs_ref[pl.ds(block, 1), :] * strain

    @pl.loop(0, INNER_BLOCKS)
    def _(block):
        elements(block, False)

    for j in range(NB):
        cell_copy(j).wait_recv()
    index = cross_ref[pl.ds(0, 8, stride=2), :]
    lanes, bits = index & 127, bit_masks(index >> 7, 4)
    index = cross_ref[pl.ds(1, 8, stride=2), :]
    ghost_lanes, ghost_bits = index & 127, bit_masks(index >> 7, 3)

    def ghost(row):
        return ghost_rows(cells_in, row, CELL_ROWS, ghost_lanes, ghost_bits)

    product = jnp.zeros((8, LANES), F32)
    for t in range(STEPS):
        product = product + (own_rows(press_ref, t, lanes, bits) - ghost(t)) * (
            own_rows(apress_ref, t, lanes, bits) - ghost(STEPS + t)
        )
    perm_a, perm_b = own_perm(perm_ref, lanes, bits), ghost(2 * STEPS)
    common = face_common(perm_a, perm_b, product)
    term_a_ref[...] = common * perm_b
    term_b_ref[...] = common * perm_a
    back_out[...] = scatter_rows(
        None, term_b_ref, NB, lambda s: cross_ref[2 * s + 1 : 2 * s + 2, :]
    )
    gradient = gradient + scatter_rows(
        None, term_a_ref, OWN, lambda s: cross_ref[2 * s : 2 * s + 1, :]
    )
    for j in range(NB):
        back_copy(j).start()

    for j in range(NB):
        node_copy(j).wait_recv()

    @pl.loop(INNER_BLOCKS, ALL_BLOCKS)
    def _(block):
        elements(block, True)

    for j in range(NB):
        back_copy(j).wait_recv()
    term_a_ref[...] = back_in[pl.ds(0, NB, stride=9), :]
    gp_ref[...] = gradient + scatter_rows(
        None, term_a_ref, OWN, lambda s: send_cells_ref[s : s + 1, :]
    )
    for j in range(NB):
        cell_copy(j).wait_send()
        node_copy(j).wait_send()
        back_copy(j).wait_send()


def on_device(
    displacement,
    adjoint_disp,
    pressure,
    adjoint_pressure,
    youngs,
    permeability,
    stiffness,
    send_nodes,
    send_cells,
    elem_nodes,
    inner_faces,
    cross_faces,
):
    count = lax.axis_size("dom")

    def components(value):
        return value.transpose(1, 0, 2).reshape(24, -1)

    def interleaved(value):
        return value.reshape(2, -1, LANES).transpose(1, 0, 2).reshape(-1, LANES)

    vmem = pl.BlockSpec(memory_space=pltpu.VMEM)
    grad_youngs, grad_perm = pl.pallas_call(
        functools.partial(kernel, count),
        out_shape=(
            jax.ShapeDtypeStruct((OWN, LANES), F32),
            jax.ShapeDtypeStruct((OWN, LANES), F32),
        ),
        in_specs=[vmem] * 12,
        out_specs=(vmem, vmem),
        scratch_shapes=[
            pltpu.VMEM((NB * CELL_ROWS, LANES), F32),
            pltpu.VMEM((NB * NODE_ROWS, LANES), F32),
            pltpu.VMEM((NB * CELL_ROWS, LANES), F32),
            pltpu.VMEM((NB * NODE_ROWS, LANES), F32),
            pltpu.VMEM((NB, LANES), F32),
            pltpu.VMEM((NB * 9, LANES), F32),
            pltpu.VMEM((8, LANES), F32),
            pltpu.VMEM((8, LANES), F32),
        ]
        + [pltpu.SemaphoreType.DMA((NB,))] * 6,
        compiler_params=pltpu.CompilerParams(collective_id=0, has_side_effects=True),
    )(
        components(displacement),
        components(adjoint_disp),
        pressure,
        adjoint_pressure,
        youngs.reshape(OWN, LANES),
        permeability.reshape(OWN, LANES),
        stiffness,
        send_nodes,
        send_cells,
        elem_nodes,
        interleaved(inner_faces),
        interleaved(cross_faces),
    )
    return grad_youngs.reshape(-1), grad_perm.reshape(-1)


def solution(mesh):
    in_specs = (
        P(None, None, "dom"),
        P(None, None, "dom"),
        P(None, "dom"),
        P(None, "dom"),
        P("dom"),
        P("dom"),
        P(),
        P(None, "dom"),
        P(None, "dom"),
        P(None, "dom"),
        P(None, "dom"),
        P(None, "dom"),
    )
    return jax.shard_map(
        on_device,
        mesh=mesh,
        in_specs=in_specs,
        out_specs=(P("dom"), P("dom")),
        check_vma=False,
    )
```

time: 875 us -> 41.2 us (0.05)
  the two profiles are of different devices: /device:TPU:24 before, /device:TPU:1 now
where the time goes in v1:
time: 41.2 us; the launch traced here: 41 us
  Pallas kernels  38.5 us (93%)
  local copies, waits for them, and re-layouts  1.9 us (5%)
  between operations  0.65 us (2%)
    pallas_call x1, Pallas kernels, on_device(): pl.pallas_call(functools.partial(kernel, count), out_shape=(jax.ShapeDtyp...  38.5 us
    unnamed x4, local copies, waits for them, and re-layouts  1.9 us

profile of v1, /device:TPU:1, one launch (start us, length us, event | category | flops | bytes accessed | tf_op | source)
XLA Modules:
  0.0 41.0 jit_solution(2661621327671838418)
XLA Ops:
  0.6 38.5 %shard_map.131 = (f32[16,128]{1,0:T(8,128)}, f32[16,128]{1,0:T(8,128)}) custom-call(f32[24,2048]{1,0:T(8,128)} %bitcast.20, f32[24,2048]{1,0:T(8,128)} %bitcast.21, f32[8,2048]{1,0:T(8,128)} %press_ref.1, f32[8,2048]{1,0:T(8,128)} %apress_ref.1, f32[16,128]{1,0:T(8,128)} %bitcast.23, f32[16,128]{1,0:T(8,128)} %bitcast.24, f32[24,24]{1,0:T(8,128)} %stiff_ref.1, ...), custom_call_target="tpu_custom_call" | custom-call | tf_op jit(solution)/shard_map/pallas_call | solution.py:330
  39.1 0.0 copy-start
  39.1 1.3 %copy.18 = f32[2048]{0:T(1024)} copy(f32[2048]{0:T(1024)} %bitcast.27) | data formatting | bytes 16384
  40.4 0.0 copy-done
  40.4 0.6 %copy.19 = f32[2048]{0:T(1024)} copy(f32[2048]{0:T(1024)S(1)} %bitcast.26) | data formatting | bytes 16384
Async XLA Ops:
  39.1 1.3 %copy-start = (f32[16,128]{1,0:T(8,128)S(1)}, f32[16,128]{1,0:T(8,128)}, u32[]{:S(2)}) copy-start(f32[16,128]{1,0:T(8,128)} %get-tuple-element.5) | copy-start | bytes 24580

commit v2 on v1

--- a/solution.py
+++ b/solution.py
@@ -20,6 +20,13 @@
 CELL_BLOCKS = 6
 INNER_BLOCKS = 12
 ALL_BLOCKS = 16
+WIDE = 256
+OWN_GROUPS = 8
+GHOST_GROUPS = 4
+GROUP = 4
+PITCH = 56
+SPAN = 16
+CROSS_AT = 3
 
 
 def take(source, lanes):
@@ -73,7 +80,7 @@
     )
 
 
-def scatter_rows(index, value_ref, rows, index_row):
+def scatter_rows(value_ref, rows, index_row):
     chunk_iota = lax.broadcasted_iota(jnp.int32, (rows, LANES), 0)
     lane_iota = lax.broadcasted_iota(jnp.int32, (LANES, LANES), 0)
     left, right = [], []
@@ -89,6 +96,47 @@
     both = jnp.concatenate([high, low], axis=0).astype(BF16)
     summed = contract_lanes(both, jnp.concatenate(right, axis=1))
     return summed[:rows] + summed[rows:]
+
+
+def table_rows(value):
+    high = value.astype(BF16)
+    low = (value - high.astype(F32)).astype(BF16)
+    return jnp.concatenate([high, low], axis=1)
+
+
+def lookup(table_ref, groups, indices):
+    place = lax.broadcasted_iota(jnp.int32, (WIDE, LANES), 0)
+    columns = []
+    for index in indices:
+        column = jnp.broadcast_to((index & (WIDE - 1))[:1], (WIDE, LANES))
+        columns.append(jnp.where(column == place, 1.0, 0.0).astype(BF16))
+    once = jnp.concatenate(columns, axis=1)
+    found = jnp.dot(
+        table_ref[: groups * NODE_ROWS, :],
+        jnp.concatenate([once, once], axis=0),
+        preferred_element_type=F32,
+    )
+    results = []
+    for n, index in enumerate(indices):
+        group = index >> 8
+        bits = bit_masks(group, 3)
+
+        def piece(h, k):
+            row = h * NODE_ROWS + 8 * k
+            return found[row : row + 8, n * LANES : (n + 1) * LANES]
+
+        pieces = []
+        for k in range(NODE_ROWS // 8):
+            value = pick([lambda h=h: piece(h, k) for h in range(OWN_GROUPS)], bits)
+            if groups > OWN_GROUPS:
+                outside = pick(
+                    [lambda h=h: piece(OWN_GROUPS + h, k) for h in range(GHOST_GROUPS)],
+                    bits,
+                )
+                value = jnp.where(group >= OWN_GROUPS, outside, value)
+            pieces.append(value)
+        results.append(pieces)
+    return results
 
 
 def face_common(perm_a, perm_b, product):
@@ -120,6 +168,9 @@
     back_in,
     term_a_ref,
     term_b_ref,
+    table_ref,
+    state_ref,
+    gradient_ref,
     cell_send,
     cell_recv,
     node_send,
@@ -129,12 +180,21 @@
 ):
     me = lax.axis_index("dom")
 
+    def on_axis(offset):
+        return (me + offset >= 0) & (me + offset < count)
+
     def at(offset):
-        return (lax.rem(me + (offset + count), count),)
+        return (me + offset,)
 
     barrier = pltpu.get_barrier_semaphore()
+    neighbours = 0
     for offset in OFFSETS:
-        pl.semaphore_signal(barrier, inc=1, device_id=at(offset), device_id_type=MESH)
+
+        @pl.when(on_axis(offset))
+        def _():
+            pl.semaphore_signal(barrier, inc=1, device_id=at(offset), device_id_type=MESH)
+
+        neighbours = neighbours + on_axis(offset).astype(jnp.int32)
 
     index = send_cells_ref[...]
     lanes, bits = index & 127, bit_masks(index >> 7, 4)
@@ -147,15 +207,31 @@
         if r == 2 * STEPS:
             permeability = own_perm(perm_ref, lanes, bits)
         cells_out[pl.ds(r, NB, stride=CELL_ROWS), :] = permeability
-    index = send_nodes_ref[...]
-    lanes, bits = index & 127, bit_masks(index >> 7, 4)
-    for r in range(24):
-        nodes_out[pl.ds(r, NB, stride=NODE_ROWS), :] = own_rows(disp_ref, r, lanes, bits)
-        nodes_out[pl.ds(24 + r, NB, stride=NODE_ROWS), :] = own_rows(
-            adj_ref, r, lanes, bits
-        )
-
-    pl.semaphore_wait(barrier, NB)
+    for h in range(OWN_GROUPS):
+        columns = slice(h * WIDE, (h + 1) * WIDE)
+        table_ref[h * NODE_ROWS : (h + 1) * NODE_ROWS, :] = table_rows(
+            jnp.concatenate([disp_ref[:, columns], adj_ref[:, columns]], axis=0)
+        )
+    for first in range(0, NB, GROUP):
+        rows = [
+            jnp.broadcast_to(send_nodes_ref[j : j + 1, :], (8, LANES))
+            for j in range(first, first + GROUP)
+        ]
+        for j, pieces in zip(range(first, first + GROUP), lookup(table_ref, OWN_GROUPS, rows)):
+            for k, value in enumerate(pieces):
+                row = j * NODE_ROWS + 8 * k
+                nodes_out[row : row + 8, :] = value
+
+    for j in range(NB):
+
+        @pl.when(jnp.logical_not(on_axis(OFFSETS[j])))
+        def _():
+            rows = slice(j * NODE_ROWS, (j + 1) * NODE_ROWS)
+            nodes_in[rows, :] = jnp.zeros((NODE_ROWS, LANES), F32)
+
+        @pl.when(jnp.logical_not(on_axis(-OFFSETS[j])))
+        def _():
+            back_in[8 * j : 8 * j + 8, :] = jnp.zeros((8, LANES), F32)
 
     def cell_copy(j):
         return pltpu.make_async_remote_copy(
@@ -187,12 +263,16 @@
             device_id_type=MESH,
         )
 
-    for j in range(NB):
-        cell_copy(j).start()
-    for j in range(NB):
-        node_copy(j).start()
-
-    def inner_faces(block, gradient):
+    def each(offset_sign, action):
+        for j in reversed(range(NB)):
+            pl.when(on_axis(offset_sign * OFFSETS[j]))(lambda j=j: action(j))
+
+    def send_states():
+        pl.semaphore_wait(barrier, neighbours)
+        each(-1, lambda j: cell_copy(j).start())
+        each(-1, lambda j: node_copy(j).start())
+
+    def inner_faces(block):
         base = pl.multiple_of(block * 16, 16)
         ends = []
         for side in range(2):
@@ -210,98 +290,106 @@
         common = face_common(ka, kb, product)
         term_a_ref[...] = common * kb
         term_b_ref[...] = common * ka
+        gradient = gradient_ref[...]
         for side, term_ref in enumerate((term_a_ref, term_b_ref)):
             gradient = gradient + scatter_rows(
-                None,
                 term_ref,
                 OWN,
                 lambda s: inner_ref[pl.ds(base + 2 * s + side, 1), :],
             )
-        return gradient
-
-    gradient = lax.fori_loop(0, CELL_BLOCKS, inner_faces, jnp.zeros((OWN, LANES), F32))
+        gradient_ref[...] = gradient
 
     stiff_high, stiff_low = split(stiff_ref[...])
     stiff = jnp.concatenate([stiff_high, stiff_low, stiff_high], axis=1).astype(BF16)
 
-    def elements(block, ghosts):
+    def elements(block, groups):
         column = pl.multiple_of(block * LANES, LANES)
-        index = elem_ref[:, pl.ds(column, LANES)]
-        lanes, chunk = index & 127, index >> 7
-        bits = bit_masks(chunk, 4)
-        outside = chunk >= OWN
-
-        def corner_rows(ref, row, ghost_row):
-            value = own_rows(ref, row, lanes, bits)
-            if ghosts:
-                value = jnp.where(
-                    outside, ghost_rows(nodes_in, ghost_row, NODE_ROWS, lanes, bits), value
-                )
-            return value
-
+        for first in range(0, 8, GROUP):
+            rows = [
+                jnp.broadcast_to(elem_ref[n : n + 1, pl.ds(column, LANES)], (8, LANES))
+                for n in range(first, first + GROUP)
+            ]
+            for n, pieces in zip(range(first, first + GROUP), lookup(table_ref, groups, rows)):
+                for k, value in enumerate(pieces):
+                    row = n * PITCH + 8 * k
+                    state_ref[row : row + 8, :] = value
         total = jnp.zeros((8, LANES), F32)
         for t in range(STEPS):
             forward = jnp.concatenate(
-                [corner_rows(disp_ref, 8 * c + t, 8 * c + t) for c in range(3)], axis=0
+                [state_ref[pl.ds(8 * c + t, 8, stride=PITCH), :] for c in range(3)], axis=0
             )
-            adjoint = [corner_rows(adj_ref, 8 * c + t, 24 + 8 * c + t) for c in range(3)]
             high, low = split(forward)
             stacked = jnp.concatenate([high, high, low], axis=0).astype(BF16)
             weighted = jnp.dot(stiff, stacked, preferred_element_type=F32)
             for c in range(3):
-                total = total + adjoint[c] * weighted[8 * c : 8 * c + 8]
+                adjoint = state_ref[pl.ds(24 + 8 * c + t, 8, stride=PITCH), :]
+                total = total + adjoint * weighted[8 * c : 8 * c + 8]
         strain = jnp.sum(total, axis=0, keepdims=True)
         gy_ref[pl.ds(block, 1), :] = -youngs_ref[pl.ds(block, 1), :] * strain
 
-    @pl.loop(0, INNER_BLOCKS)
-    def _(block):
-        elements(block, False)
-
-    for j in range(NB):
-        cell_copy(j).wait_recv()
-    index = cross_ref[pl.ds(0, 8, stride=2), :]
-    lanes, bits = index & 127, bit_masks(index >> 7, 4)
-    index = cross_ref[pl.ds(1, 8, stride=2), :]
-    ghost_lanes, ghost_bits = index & 127, bit_masks(index >> 7, 3)
-
-    def ghost(row):
-        return ghost_rows(cells_in, row, CELL_ROWS, ghost_lanes, ghost_bits)
-
-    product = jnp.zeros((8, LANES), F32)
-    for t in range(STEPS):
-        product = product + (own_rows(press_ref, t, lanes, bits) - ghost(t)) * (
-            own_rows(apress_ref, t, lanes, bits) - ghost(STEPS + t)
-        )
-    perm_a, perm_b = own_perm(perm_ref, lanes, bits), ghost(2 * STEPS)
-    common = face_common(perm_a, perm_b, product)
-    term_a_ref[...] = common * perm_b
-    term_b_ref[...] = common * perm_a
-    back_out[...] = scatter_rows(
-        None, term_b_ref, NB, lambda s: cross_ref[2 * s + 1 : 2 * s + 2, :]
-    )
-    gradient = gradient + scatter_rows(
-        None, term_a_ref, OWN, lambda s: cross_ref[2 * s : 2 * s + 1, :]
-    )
-    for j in range(NB):
-        back_copy(j).start()
-
-    for j in range(NB):
-        node_copy(j).wait_recv()
+    def shared_faces():
+        each(1, lambda j: cell_copy(j).wait_recv())
+        index = cross_ref[pl.ds(0, 8, stride=2), :]
+        lanes, bits = index & 127, bit_masks(index >> 7, 4)
+        index = cross_ref[pl.ds(1, 8, stride=2), :]
+        ghost_lanes, ghost_bits = index & 127, bit_masks(index >> 7, 3)
+
+        def ghost(row):
+            return ghost_rows(cells_in, row, CELL_ROWS, ghost_lanes, ghost_bits)
+
+        product = jnp.zeros((8, LANES), F32)
+        for t in range(STEPS):
+            product = product + (own_rows(press_ref, t, lanes, bits) - ghost(t)) * (
+                own_rows(apress_ref, t, lanes, bits) - ghost(STEPS + t)
+            )
+        perm_a, perm_b = own_perm(perm_ref, lanes, bits), ghost(2 * STEPS)
+        common = face_common(perm_a, perm_b, product)
+        term_a_ref[...] = common * perm_b
+        term_b_ref[...] = common * perm_a
+        back_out[...] = scatter_rows(
+            term_b_ref, NB, lambda s: cross_ref[2 * s + 1 : 2 * s + 2, :]
+        )
+        gradient_ref[...] += scatter_rows(
+            term_a_ref, OWN, lambda s: cross_ref[2 * s : 2 * s + 1, :]
+        )
+        each(1, lambda j: back_copy(j).start())
+
+    gradient_ref[...] = jnp.zeros((OWN, LANES), F32)
+    early = lax.rem(me, SPAN) < SPAN // 2
+    send_at = jnp.where(early, CELL_BLOCKS, 0)
+    cross_at = jnp.where(early, CELL_BLOCKS, CROSS_AT)
+
+    @pl.loop(0, CELL_BLOCKS + 1)
+    def _(step):
+        pl.when(step == send_at)(send_states)
+        pl.when(step == cross_at)(shared_faces)
+
+        @pl.when(step < CELL_BLOCKS)
+        def _():
+            elements(2 * step, OWN_GROUPS)
+            elements(2 * step + 1, OWN_GROUPS)
+            inner_faces(step)
+
+    each(1, lambda j: node_copy(j).wait_recv())
+    for h in range(GHOST_GROUPS):
+        row = (OWN_GROUPS + h) * NODE_ROWS
+        ghosts = [
+            nodes_in[j * NODE_ROWS : (j + 1) * NODE_ROWS, :] for j in (2 * h, 2 * h + 1)
+        ]
+        table_ref[row : row + NODE_ROWS, :] = table_rows(jnp.concatenate(ghosts, axis=1))
 
     @pl.loop(INNER_BLOCKS, ALL_BLOCKS)
     def _(block):
-        elements(block, True)
-
-    for j in range(NB):
-        back_copy(j).wait_recv()
+        elements(block, OWN_GROUPS + GHOST_GROUPS)
+
+    each(-1, lambda j: back_copy(j).wait_recv())
     term_a_ref[...] = back_in[pl.ds(0, NB, stride=9), :]
-    gp_ref[...] = gradient + scatter_rows(
-        None, term_a_ref, OWN, lambda s: send_cells_ref[s : s + 1, :]
-    )
-    for j in range(NB):
-        cell_copy(j).wait_send()
-        node_copy(j).wait_send()
-        back_copy(j).wait_send()
+    gp_ref[...] = gradient_ref[...] + scatter_rows(
+        term_a_ref, OWN, lambda s: send_cells_ref[s : s + 1, :]
+    )
+    each(-1, lambda j: cell_copy(j).wait_send())
+    each(-1, lambda j: node_copy(j).wait_send())
+    each(1, lambda j: back_copy(j).wait_send())
 
 
 def on_device(
@@ -344,6 +432,9 @@
             pltpu.VMEM((NB * 9, LANES), F32),
             pltpu.VMEM((8, LANES), F32),
             pltpu.VMEM((8, LANES), F32),
+            pltpu.VMEM(((OWN_GROUPS + GHOST_GROUPS) * NODE_ROWS, 2 * WIDE), BF16),
+            pltpu.VMEM((8 * PITCH, LANES), F32),
+            pltpu.VMEM((OWN, LANES), F32),
         ]
         + [pltpu.SemaphoreType.DMA((NB,))] * 6,
         compiler_params=pltpu.CompilerParams(collective_id=0, has_side_effects=True),

time: 41.2 us -> 32.7 us (0.79)
  the two profiles are of different devices: /device:TPU:1 before, /device:TPU:24 now
where the time goes in v2:
time: 32.7 us; the launch traced here: 32.6 us
  Pallas kernels  30 us (92%)
  local copies, waits for them, and re-layouts  1.9 us (6%)
  between operations  0.65 us (2%)
    pallas_call x1, Pallas kernels, on_device(): pl.pallas_call(functools.partial(kernel, count), out_shape=(jax.ShapeDtyp...  30 us
    unnamed x4, local copies, waits for them, and re-layouts  1.9 us

profile of v2, /device:TPU:24, one launch (start us, length us, event | category | flops | bytes accessed | tf_op | source)
XLA Modules:
  0.0 32.6 jit_solution(9453742305393113450)
XLA Ops:
  0.6 30.0 %shard_map.131 = (f32[16,128]{1,0:T(8,128)}, f32[16,128]{1,0:T(8,128)}) custom-call(f32[24,2048]{1,0:T(8,128)} %bitcast.20, f32[24,2048]{1,0:T(8,128)} %bitcast.21, f32[8,2048]{1,0:T(8,128)} %press_ref.1, f32[8,2048]{1,0:T(8,128)} %apress_ref.1, f32[16,128]{1,0:T(8,128)} %bitcast.23, f32[16,128]{1,0:T(8,128)} %bitcast.24, f32[24,24]{1,0:T(8,128)} %stiff_ref.1, ...), custom_call_target="tpu_custom_call" | custom-call | tf_op jit(solution)/shard_map/pallas_call | solution.py:418
  30.7 0.0 copy-start
  30.7 1.3 %copy.18 = f32[2048]{0:T(1024)} copy(f32[2048]{0:T(1024)} %bitcast.27) | data formatting | bytes 16384
  32.0 0.0 copy-done
  32.0 0.6 %copy.19 = f32[2048]{0:T(1024)} copy(f32[2048]{0:T(1024)S(1)} %bitcast.26) | data formatting | bytes 16384
Async XLA Ops:
  30.7 1.3 %copy-start = (f32[16,128]{1,0:T(8,128)S(1)}, f32[16,128]{1,0:T(8,128)}, u32[]{:S(2)}) copy-start(f32[16,128]{1,0:T(8,128)} %get-tuple-element.5) | copy-start | bytes 24580

commit v3 on v2

v3 whole, which is shorter than its diff:
```python
import functools

import jax
import jax.numpy as jnp
from jax import lax
from jax.experimental import pallas as pl
from jax.experimental.pallas import tpu as pltpu
from jax.sharding import PartitionSpec as P

OFFSETS = (1, -1, 2, -2, 4, -4, 8, -8)
MESH = pl.DeviceIdType.MESH
F32 = jnp.float32
BF16 = jnp.bfloat16
LANES = 128
STEPS = 8
OWN = 16
NB = 8
CELL_ROWS = 16
NODE_ROWS = 48
CELL_BLOCKS = 6
INNER_BLOCKS = 12
EDGE_BLOCKS = 4
WIDE = 256
OWN_GROUPS = 8
GHOST_GROUPS = 4
GROUP = 4
PITCH = 56
SPAN = 16
ROW = 64
EARLIEST = 4
CROSS_AFTER = 5


def take(source, lanes):
    return jnp.take_along_axis(source, lanes, axis=1, mode="promise_in_bounds")


def pick(values, bits):
    if len(values) == 1:
        return values[0]()
    half = len(values) // 2
    top = bits[half.bit_length() - 1]
    low = pick(values[:half], bits)
    high = pick(values[half:], bits)
    return jnp.where(top, high, low)


def wide(row):
    return jnp.broadcast_to(row, (8, LANES))


def bit_masks(chunk, count):
    return [(chunk & (1 << bit)) != 0 for bit in range(count)]


def own_rows(ref, row, lanes, bits):
    return pick(
        [
            lambda h=h: take(wide(ref[row : row + 1, h * LANES : (h + 1) * LANES]), lanes)
            for h in range(OWN)
        ],
        bits,
    )


def own_perm(ref, lanes, bits):
    return pick(
        [lambda h=h: take(wide(ref[h : h + 1, :]), lanes) for h in range(OWN)], bits
    )


def ghost_rows(rows, lanes, bits):
    return pick([lambda j=j: take(wide(rows(j)), lanes) for j in range(NB)], bits)


def split(value):
    high = value.astype(BF16).astype(F32)
    return high, value - high


def small(column):
    column = column.astype(F32)
    return jnp.concatenate([column, column], axis=0).astype(BF16)


def lane_marks(place_ref, index_row):
    one, zero = jnp.ones((16, LANES), BF16), jnp.zeros((16, LANES), BF16)
    columns = []
    for s in range(8):
        lane = small(wide(index_row(s)) & (LANES - 1))
        columns.append(
            jnp.concatenate(
                [
                    jnp.where(lane == place_ref[row : row + 16, :], one, zero)
                    for row in range(0, LANES, 16)
                ],
                axis=0,
            )
        )
    return jnp.concatenate(columns, axis=1)


def scatter_rows(marks, value_ref, rows, index_row):
    chunk_iota = lax.broadcasted_iota(jnp.int32, (rows, LANES), 0)
    left = []
    for s in range(8):
        value = jnp.broadcast_to(value_ref[s : s + 1, :], (rows, LANES))
        chunk = jnp.concatenate([wide(index_row(s)) >> 7] * (rows // 8), axis=0)
        left.append(jnp.where(chunk == chunk_iota, value, 0.0))
    high, low = split(jnp.concatenate(left, axis=1))
    summed = lax.dot_general(
        jnp.concatenate([high, low], axis=0).astype(BF16),
        marks,
        (((1,), (1,)), ((), ())),
        preferred_element_type=F32,
    )
    return summed[:rows] + summed[rows:]


def fill_table(table_ref, row, value):
    high = value.astype(BF16)
    low = (value - high.astype(F32)).astype(BF16)
    for half in range(2):
        columns = slice(half * LANES, (half + 1) * LANES)
        table_ref[half, row : row + NODE_ROWS, :] = high[:, columns]
        table_ref[2 + half, row : row + NODE_ROWS, :] = low[:, columns]


def mark(place_ref, once_ref, slot, indices):
    one, zero = jnp.ones((16, LANES), BF16), jnp.zeros((16, LANES), BF16)
    for n, index in enumerate(indices):
        column = small(index & (WIDE - 1))
        for row in range(0, WIDE, 16):
            match = column == place_ref[row : row + 16, :]
            once_ref[slot, n, row : row + 16, :] = jnp.where(match, one, zero)


def lookup(table_ref, first, groups, once_ref, slot, indices):
    once = jnp.concatenate([once_ref[slot, n] for n in range(len(indices))], axis=1)
    rows = slice(first * NODE_ROWS, (first + groups) * NODE_ROWS)
    found = sum(
        jnp.dot(
            jnp.concatenate([table_ref[plane, rows, :], table_ref[plane + 1, rows, :]], axis=1),
            once,
            preferred_element_type=F32,
        )
        for plane in (0, 2)
    )
    results = []
    for n, index in enumerate(indices):
        bits = bit_masks(index >> 8, 3)

        def piece(h, k):
            row = h * NODE_ROWS + 8 * k
            return found[row : row + 8, n * LANES : (n + 1) * LANES]

        results.append(
            [
                pick([lambda h=h: piece(h, k) for h in range(groups)], bits)
                for k in range(NODE_ROWS // 8)
            ]
        )
    return results


def face_common(perm_a, perm_b, product):
    both = perm_a + perm_b
    return 2.0 * perm_a * perm_b * product / (both * both)


def kernel(
    count,
    disp_hbm,
    adj_hbm,
    press_hbm,
    apress_hbm,
    youngs_hbm,
    perm_hbm,
    stiff_hbm,
    send_nodes_hbm,
    send_cells_hbm,
    elem_hbm,
    inner_hbm,
    cross_hbm,
    gy_ref,
    gp_ref,
    disp_ref,
    adj_ref,
    press_ref,
    apress_ref,
    youngs_ref,
    perm_ref,
    stiff_ref,
    send_nodes_ref,
    send_cells_ref,
    elem_ref,
    inner_ref,
    cross_ref,
    cells_out,
    perms_out,
    nodes_out,
    cells_in,
    perms_in,
    nodes_in,
    back_out,
    back_in,
    term_a_ref,
    term_b_ref,
    edge_ref,
    face_ref,
    back_marks_ref,
    table_ref,
    place_ref,
    once_ref,
    edge_once_ref,
    state_ref,
    edge_state_ref,
    gradient_ref,
    cell_send,
    cell_recv,
    perm_send,
    perm_recv,
    node_send,
    node_recv,
    back_send,
    back_recv,
    stage_sem,
):
    me = lax.axis_index("dom")

    def on_axis(offset):
        return (me + offset >= 0) & (me + offset < count)

    barrier = pltpu.get_barrier_semaphore()
    neighbours = 0
    for offset in OFFSETS:

        @pl.when(on_axis(offset))
        def _():
            pl.semaphore_signal(
                barrier, inc=1, device_id=(me + offset,), device_id_type=MESH
            )

        neighbours = neighbours + on_axis(offset).astype(jnp.int32)

    staged = (
        (send_cells_hbm, send_cells_ref),
        (press_hbm, press_ref),
        (apress_hbm, apress_ref),
        (perm_hbm, perm_ref),
        (send_nodes_hbm, send_nodes_ref),
        (disp_hbm, disp_ref),
        (adj_hbm, adj_ref),
        (elem_hbm, elem_ref),
        (inner_hbm, inner_ref),
        (stiff_hbm, stiff_ref),
        (youngs_hbm, youngs_ref),
        (cross_hbm, cross_ref),
    )
    stages = [
        pltpu.make_async_copy(source, target, stage_sem.at[i])
        for i, (source, target) in enumerate(staged)
    ]
    for stage in stages:
        stage.start()

    def send(source, target, send_sem, recv_sem, j, offset):
        return pltpu.make_async_remote_copy(
            src_ref=source,
            dst_ref=target,
            send_sem=send_sem.at[j],
            recv_sem=recv_sem.at[j],
            device_id=(me + offset,),
            device_id_type=MESH,
        )

    def cell_copy(j):
        rows = pl.ds(j * CELL_ROWS, CELL_ROWS)
        return send(cells_out.at[rows], cells_in.at[rows], cell_send, cell_recv, j, -OFFSETS[j])

    def perm_copy(j):
        return send(perms_out.at[j], perms_in.at[j], perm_send, perm_recv, j, -OFFSETS[j])

    def node_copy(j):
        rows = pl.ds(j * NODE_ROWS, NODE_ROWS)
        return send(nodes_out.at[rows], nodes_in.at[rows], node_send, node_recv, j, -OFFSETS[j])

    def back_copy(j):
        return send(back_out.at[j], back_in.at[j], back_send, back_recv, j, OFFSETS[j])

    def each(sign, action):
        for j in reversed(range(NB)):
            pl.when(on_axis(sign * OFFSETS[j]))(lambda j=j: action(j))

    place = lax.broadcasted_iota(jnp.int32, (WIDE, LANES), 0)
    place_ref[...] = place.astype(F32).astype(BF16)
    gradient_ref[...] = jnp.zeros((OWN, LANES), F32)
    term_a_ref[...] = jnp.zeros((8, LANES), F32)
    term_b_ref[...] = jnp.zeros((8, LANES), F32)
    state_ref[...] = jnp.zeros(state_ref.shape, F32)
    for j in range(NB):

        @pl.when(jnp.logical_not(on_axis(OFFSETS[j])))
        def _():
            rows = slice(j * NODE_ROWS, (j + 1) * NODE_ROWS)
            nodes_in[rows, :] = jnp.zeros((NODE_ROWS, LANES), F32)

        @pl.when(jnp.logical_not(on_axis(-OFFSETS[j])))
        def _():
            back_in[j] = jnp.zeros((1, LANES), F32)

    for stage in stages:
        stage.wait()

    index = send_cells_ref[...]
    lanes, bits = index & 127, bit_masks(index >> 7, 4)
    for t in range(STEPS):
        cells_out[pl.ds(t, NB, stride=CELL_ROWS), :] = own_rows(press_ref, t, lanes, bits)
        cells_out[pl.ds(STEPS + t, NB, stride=CELL_ROWS), :] = own_rows(
            apress_ref, t, lanes, bits
        )
    permeability = own_perm(perm_ref, lanes, bits)
    for j in range(NB):
        perms_out[j] = permeability[j : j + 1, :]
    for h in range(OWN_GROUPS):
        columns = slice(h * WIDE, (h + 1) * WIDE)
        fill_table(
            table_ref,
            h * NODE_ROWS,
            jnp.concatenate([disp_ref[:, columns], adj_ref[:, columns]], axis=0),
        )
    for first in range(0, NB, GROUP):
        rows = [wide(send_nodes_ref[j : j + 1, :]) for j in range(first, first + GROUP)]
        slot = first // GROUP
        mark(place_ref, once_ref, slot, rows)
        found = lookup(table_ref, 0, OWN_GROUPS, once_ref, slot, rows)
        for j, pieces in zip(range(first, first + GROUP), found):
            for k, value in enumerate(pieces):
                row = j * NODE_ROWS + 8 * k
                nodes_out[row : row + 8, :] = value

    def send_states():
        pl.semaphore_wait(barrier, neighbours)

        def start_cells(j):
            cell_copy(j).start()
            perm_copy(j).start()

        each(-1, start_cells)
        each(-1, lambda j: node_copy(j).start())

    def gather_inner(block):
        base = pl.multiple_of(block * 16, 16)
        ends = []
        for side in range(2):
            index = inner_ref[pl.ds(base + side, 8, stride=2), :]
            lanes, bits = index & 127, bit_masks(index >> 7, 4)
            ends.append(
                (
                    [own_rows(press_ref, t, lanes, bits) for t in range(STEPS)],
                    [own_rows(apress_ref, t, lanes, bits) for t in range(STEPS)],
                    own_perm(perm_ref, lanes, bits),
                )
            )
        (pa, qa, ka), (pb, qb, kb) = ends
        product = sum((pa[t] - pb[t]) * (qa[t] - qb[t]) for t in range(STEPS))
        common = face_common(ka, kb, product)
        term_a_ref[...] = common * kb
        term_b_ref[...] = common * ka

    def scatter_inner(block):
        base = pl.multiple_of(block * 16, 16)
        gradient = gradient_ref[...]
        for side, term_ref in enumerate((term_a_ref, term_b_ref)):
            index_row = lambda s: inner_ref[pl.ds(base + 2 * s + side, 1), :]
            marks = lane_marks(place_ref, index_row)
            gradient = gradient + scatter_rows(marks, term_ref, OWN, index_row)
        gradient_ref[...] = gradient

    stiff_high, stiff_low = split(stiff_ref[...])
    stiff = jnp.concatenate([stiff_high, stiff_low, stiff_high], axis=1).astype(BF16)

    def element_rows(block, first):
        column = pl.multiple_of(block * LANES, LANES)
        return [
            wide(elem_ref[n : n + 1, pl.ds(column, LANES)]) for n in range(first, first + GROUP)
        ]

    def own_states(block, once, states, slot):
        for first in range(0, 8, GROUP):
            rows = element_rows(block, first)
            part = 2 * slot + first // GROUP
            mark(place_ref, once, part, rows)
            found = lookup(table_ref, 0, OWN_GROUPS, once, part, rows)
            for n, pieces in zip(range(first, first + GROUP), found):
                for k, value in enumerate(pieces):
                    row = n * PITCH + 8 * k
                    states[slot, row : row + 8, :] = value

    def ghost_states(block, slot):
        for first in range(0, 8, GROUP):
            rows = element_rows(block, first)
            part = 2 * slot + first // GROUP
            found = lookup(table_ref, OWN_GROUPS, GHOST_GROUPS, edge_once_ref, part, rows)
            for n, index, pieces in zip(range(first, first + GROUP), rows, found):
                outside = index >= OWN * LANES
                for k, value in enumerate(pieces):
                    row = n * PITCH + 8 * k
                    edge_state_ref[slot, row : row + 8, :] = jnp.where(
                        outside, value, edge_state_ref[slot, row : row + 8, :]
                    )

    def strain(block, states, slot):
        total = jnp.zeros((8, LANES), F32)
        for t in range(0, STEPS, 2):
            forward = jnp.concatenate(
                [
                    jnp.concatenate(
                        [states[slot, pl.ds(8 * c + u, 8, stride=PITCH), :] for c in range(3)],
                        axis=0,
                    )
                    for u in (t, t + 1)
                ],
                axis=1,
            )
            high, low = split(forward)
            stacked = jnp.concatenate([high, high, low], axis=0).astype(BF16)
            weighted = jnp.dot(stiff, stacked, preferred_element_type=F32)
            for u in range(2):
                for c in range(3):
                    adjoint = states[slot, pl.ds(24 + 8 * c + t + u, 8, stride=PITCH), :]
                    total = total + adjoint * weighted[
                        8 * c : 8 * c + 8, u * LANES : (u + 1) * LANES
                    ]
        summed = jnp.sum(total, axis=0, keepdims=True)
        gy_ref[pl.ds(block, 1), :] = -youngs_ref[pl.ds(block, 1), :] * summed

    def shared_faces():
        index = cross_ref[pl.ds(0, 8, stride=2), :]
        lanes, bits = index & 127, bit_masks(index >> 7, 4)
        for t in range(STEPS):
            face_ref[t] = own_rows(press_ref, t, lanes, bits)
            face_ref[STEPS + t] = own_rows(apress_ref, t, lanes, bits)
        perm_a = own_perm(perm_ref, lanes, bits)
        index = cross_ref[pl.ds(1, 8, stride=2), :]
        ghost_lanes, ghost_bits = index & 127, bit_masks(index >> 7, 3)

        def ghost(row):
            return ghost_rows(
                lambda j: cells_in[j * CELL_ROWS + row : j * CELL_ROWS + row + 1, :],
                ghost_lanes,
                ghost_bits,
            )

        ghost_index = lambda s: cross_ref[2 * s + 1 : 2 * s + 2, :]
        own_index = lambda s: cross_ref[2 * s : 2 * s + 1, :]
        back_marks_ref[...] = lane_marks(place_ref, ghost_index)

        def wait_cells(j):
            cell_copy(j).wait_recv()
            perm_copy(j).wait_recv()

        each(1, wait_cells)
        product = jnp.zeros((8, LANES), F32)
        for t in range(STEPS):
            product = product + (face_ref[t] - ghost(t)) * (
                face_ref[STEPS + t] - ghost(STEPS + t)
            )
        perm_b = ghost_rows(lambda j: perms_in[j], ghost_lanes, ghost_bits)
        common = face_common(perm_a, perm_b, product)
        edge_ref[0] = common * perm_b
        edge_ref[1] = common * perm_a
        returned = scatter_rows(back_marks_ref[...], edge_ref.at[1], NB, ghost_index)
        for j in range(NB):
            back_out[j] = returned[j : j + 1, :]
        each(1, lambda j: back_copy(j).start())
        gradient_ref[...] += scatter_rows(
            lane_marks(place_ref, own_index), edge_ref.at[0], OWN, own_index
        )

    place_z = lax.rem(me, SPAN) // 2
    early = place_z < SPAN // 4
    row_start = (me >= ROW) & (lax.rem(me, ROW) < SPAN)
    send_at = jnp.where(early, EARLIEST - place_z + row_start.astype(jnp.int32), 0)
    cross_at = jnp.minimum(send_at + CROSS_AFTER, CELL_BLOCKS)

    @pl.loop(0, CELL_BLOCKS)
    def _(step):
        pl.when(step == send_at)(send_states)
        pl.when(step == cross_at)(shared_faces)
        before = jnp.maximum(step - 1, 0)
        strain(2 * before, state_ref, 0)
        strain(2 * before + 1, state_ref, 1)
        scatter_inner(before)
        own_states(2 * step, once_ref, state_ref, 0)
        own_states(2 * step + 1, once_ref, state_ref, 1)
        gather_inner(step)

    strain(INNER_BLOCKS - 2, state_ref, 0)
    strain(INNER_BLOCKS - 1, state_ref, 1)
    scatter_inner(CELL_BLOCKS - 1)
    for slot in range(EDGE_BLOCKS):
        own_states(INNER_BLOCKS + slot, edge_once_ref, edge_state_ref, slot)
    pl.when(send_at == CELL_BLOCKS)(send_states)
    pl.when(cross_at == CELL_BLOCKS)(shared_faces)

    each(1, lambda j: node_copy(j).wait_recv())
    for h in range(GHOST_GROUPS):
        row = (OWN_GROUPS + h) * NODE_ROWS
        ghosts = [
            nodes_in[j * NODE_ROWS : (j + 1) * NODE_ROWS, :] for j in (2 * h, 2 * h + 1)
        ]
        fill_table(table_ref, row, jnp.concatenate(ghosts, axis=1))
    for slot in range(EDGE_BLOCKS):
        ghost_states(INNER_BLOCKS + slot, slot)
    for slot in range(EDGE_BLOCKS):
        strain(INNER_BLOCKS + slot, edge_state_ref, slot)

    cell_index = lambda s: send_cells_ref[s : s + 1, :]
    back_marks_ref[...] = lane_marks(place_ref, cell_index)
    each(-1, lambda j: back_copy(j).wait_recv())
    edge_ref[0] = jnp.concatenate([back_in[j] for j in range(NB)], axis=0)
    gp_ref[...] = gradient_ref[...] + scatter_rows(
        back_marks_ref[...], edge_ref.at[0], OWN, cell_index
    )
    each(-1, lambda j: cell_copy(j).wait_send())
    each(-1, lambda j: perm_copy(j).wait_send())
    each(-1, lambda j: node_copy(j).wait_send())
    each(1, lambda j: back_copy(j).wait_send())


def on_device(
    displacement,
    adjoint_disp,
    pressure,
    adjoint_pressure,
    youngs,
    permeability,
    stiffness,
    send_nodes,
    send_cells,
    elem_nodes,
    inner_faces,
    cross_faces,
):
    count = lax.axis_size("dom")

    def components(value):
        return value.transpose(1, 0, 2).reshape(24, -1)

    def interleaved(value):
        return value.reshape(2, -1, LANES).transpose(1, 0, 2).reshape(-1, LANES)

    vmem = pl.BlockSpec(memory_space=pltpu.VMEM)
    grad_youngs, grad_perm = pl.pallas_call(
        functools.partial(kernel, count),
        out_shape=(
            jax.ShapeDtypeStruct((OWN, LANES), F32),
            jax.ShapeDtypeStruct((OWN, LANES), F32),
        ),
        in_specs=[pl.BlockSpec(memory_space=pltpu.HBM)] * 12,
        out_specs=(vmem, vmem),
        scratch_shapes=[
            pltpu.VMEM((24, OWN * LANES), F32),
            pltpu.VMEM((24, OWN * LANES), F32),
            pltpu.VMEM((STEPS, OWN * LANES), F32),
            pltpu.VMEM((STEPS, OWN * LANES), F32),
            pltpu.VMEM((OWN, LANES), F32),
            pltpu.VMEM((OWN, LANES), F32),
            pltpu.VMEM((24, 24), F32),
            pltpu.VMEM((NB, LANES), jnp.int32),
            pltpu.VMEM((NB, LANES), jnp.int32),
            pltpu.VMEM((8, OWN * LANES), jnp.int32),
            pltpu.VMEM((16 * CELL_BLOCKS, LANES), jnp.int32),
            pltpu.VMEM((16, LANES), jnp.int32),
            pltpu.VMEM((NB * CELL_ROWS, LANES), F32),
            pltpu.VMEM((NB, 1, LANES), F32),
            pltpu.VMEM((NB * NODE_ROWS, LANES), F32),
            pltpu.VMEM((NB * CELL_ROWS, LANES), F32),
            pltpu.VMEM((NB, 1, LANES), F32),
            pltpu.VMEM((NB * NODE_ROWS, LANES), F32),
            pltpu.VMEM((NB, 1, LANES), F32),
            pltpu.VMEM((NB, 1, LANES), F32),
            pltpu.VMEM((8, LANES), F32),
            pltpu.VMEM((8, LANES), F32),
            pltpu.VMEM((2, 8, LANES), F32),
            pltpu.VMEM((2 * STEPS, 8, LANES), F32),
            pltpu.VMEM((LANES, 8 * LANES), BF16),
            pltpu.VMEM((4, (OWN_GROUPS + GHOST_GROUPS) * NODE_ROWS, LANES), BF16),
            pltpu.VMEM((WIDE, LANES), BF16),
            pltpu.VMEM((4, GROUP, WIDE, LANES), BF16),
            pltpu.VMEM((2 * EDGE_BLOCKS, GROUP, WIDE, LANES), BF16),
            pltpu.VMEM((2, 8 * PITCH, LANES), F32),
            pltpu.VMEM((EDGE_BLOCKS, 8 * PITCH, LANES), F32),
            pltpu.VMEM((OWN, LANES), F32),
        ]
        + [pltpu.SemaphoreType.DMA((NB,))] * 8
        + [pltpu.SemaphoreType.DMA((12,))],
        compiler_params=pltpu.CompilerParams(collective_id=0, has_side_effects=True),
    )(
        components(displacement),
        components(adjoint_disp),
        pressure,
        adjoint_pressure,
        youngs.reshape(OWN, LANES),
        permeability.reshape(OWN, LANES),
        stiffness,
        send_nodes,
        send_cells,
        elem_nodes,
        interleaved(inner_faces),
        interleaved(cross_faces),
    )
    return grad_youngs.reshape(-1), grad_perm.reshape(-1)


def solution(mesh):
    in_specs = (
        P(None, None, "dom"),
        P(None, None, "dom"),
        P(None, "dom"),
        P(None, "dom"),
        P("dom"),
        P("dom"),
        P(),
        P(None, "dom"),
        P(None, "dom"),
        P(None, "dom"),
        P(None, "dom"),
        P(None, "dom"),
    )
    return jax.shard_map(
        on_device,
        mesh=mesh,
        in_specs=in_specs,
        out_specs=(P("dom"), P("dom")),
        check_vma=False,
    )
```

time: 32.7 us -> 27 us (0.83)
  Pallas kernels: 30 us -> 24.3 us
    pallas_call x1, Pallas kernels: 30 us -> 24.3 us  [on_device(): pl.pallas_call(functools.partial(kernel, count), out_shape=(jax.ShapeDtyp...]
where the time goes in v3:
time: 27 us; the launch traced here: 26.9 us
  Pallas kernels  24.3 us (90%)
  local copies, waits for them, and re-layouts  1.9 us (7%)
  between operations  0.65 us (2%)
    pallas_call x1, Pallas kernels, on_device(): pl.pallas_call(functools.partial(kernel, count), out_shape=(jax.ShapeDtyp...  24.3 us
    unnamed x4, local copies, waits for them, and re-layouts  1.9 us

profile of v3, /device:TPU:24, one launch (start us, length us, event | category | flops | bytes accessed | tf_op | source)
XLA Modules:
  0.0 26.9 jit_solution(202293605871773441)
XLA Ops:
  0.6 24.3 %shard_map.131 = (f32[16,128]{1,0:T(8,128)}, f32[16,128]{1,0:T(8,128)}) custom-call(f32[24,2048]{1,0:T(8,128)} %bitcast.20, f32[24,2048]{1,0:T(8,128)} %bitcast.21, f32[8,2048]{1,0:T(8,128)} %press_hbm.1, f32[8,2048]{1,0:T(8,128)} %apress_hbm.1, f32[16,128]{1,0:T(8,128)} %bitcast.23, f32[16,128]{1,0:T(8,128)} %bitcast.24, f32[24,24]{1,0:T(8,128)} %stiff_hbm.1, ...), custom_call_target="tpu_custom_call" | custom-call | tf_op jit(solution)/shard_map/pallas_call | solution.py:555
  24.9 0.0 copy-start
  25.0 1.3 %copy.18 = f32[2048]{0:T(1024)} copy(f32[2048]{0:T(1024)} %bitcast.27) | data formatting | bytes 16384
  26.3 0.0 copy-done
  26.3 0.6 %copy.19 = f32[2048]{0:T(1024)} copy(f32[2048]{0:T(1024)S(1)} %bitcast.26) | data formatting | bytes 16384
Async XLA Ops:
  24.9 1.3 %copy-start = (f32[16,128]{1,0:T(8,128)S(1)}, f32[16,128]{1,0:T(8,128)}, u32[]{:S(2)}) copy-start(f32[16,128]{1,0:T(8,128)} %get-tuple-element.5) | copy-start | bytes 24580

commit v4 on v3

--- a/solution.py
+++ b/solution.py
@@ -28,7 +28,7 @@
 SPAN = 16
 ROW = 64
 EARLIEST = 4
-CROSS_AFTER = 5
+CROSS_AFTER = 4
 
 
 def take(source, lanes):
@@ -182,8 +182,7 @@
     elem_hbm,
     inner_hbm,
     cross_hbm,
-    gy_ref,
-    gp_ref,
+    out_ref,
     disp_ref,
     adj_ref,
     press_ref,
@@ -233,7 +232,7 @@
 
     barrier = pltpu.get_barrier_semaphore()
     neighbours = 0
-    for offset in OFFSETS:
+    for offset in reversed(OFFSETS):
 
         @pl.when(on_axis(offset))
         def _():
@@ -433,7 +432,7 @@
                         8 * c : 8 * c + 8, u * LANES : (u + 1) * LANES
                     ]
         summed = jnp.sum(total, axis=0, keepdims=True)
-        gy_ref[pl.ds(block, 1), :] = -youngs_ref[pl.ds(block, 1), :] * summed
+        out_ref[pl.ds(block, 1), :] = -youngs_ref[pl.ds(block, 1), :] * summed
 
     def shared_faces():
         index = cross_ref[pl.ds(0, 8, stride=2), :]
@@ -520,7 +519,7 @@
     back_marks_ref[...] = lane_marks(place_ref, cell_index)
     each(-1, lambda j: back_copy(j).wait_recv())
     edge_ref[0] = jnp.concatenate([back_in[j] for j in range(NB)], axis=0)
-    gp_ref[...] = gradient_ref[...] + scatter_rows(
+    out_ref[OWN:, :] = gradient_ref[...] + scatter_rows(
         back_marks_ref[...], edge_ref.at[0], OWN, cell_index
     )
     each(-1, lambda j: cell_copy(j).wait_send())
@@ -552,14 +551,11 @@
         return value.reshape(2, -1, LANES).transpose(1, 0, 2).reshape(-1, LANES)
 
     vmem = pl.BlockSpec(memory_space=pltpu.VMEM)
-    grad_youngs, grad_perm = pl.pallas_call(
+    gradients = pl.pallas_call(
         functools.partial(kernel, count),
-        out_shape=(
-            jax.ShapeDtypeStruct((OWN, LANES), F32),
-            jax.ShapeDtypeStruct((OWN, LANES), F32),
-        ),
+        out_shape=pltpu.VMEM((2 * OWN, LANES), F32),
         in_specs=[pl.BlockSpec(memory_space=pltpu.HBM)] * 12,
-        out_specs=(vmem, vmem),
+        out_specs=vmem,
         scratch_shapes=[
             pltpu.VMEM((24, OWN * LANES), F32),
             pltpu.VMEM((24, OWN * LANES), F32),
@@ -611,7 +607,7 @@
         interleaved(inner_faces),
         interleaved(cross_faces),
     )
-    return grad_youngs.reshape(-1), grad_perm.reshape(-1)
+    return gradients[:OWN].reshape(-1), gradients[OWN:].reshape(-1)
 
 
 def solution(mesh):

time: 27 us -> 25 us (0.926)
  local copies, waits for them, and re-layouts: 1.9 us -> 0.61 us
  Pallas kernels: 24.3 us -> 23.7 us
    unnamed x4 -> x0, local copies, waits for them, and re-layouts: 1.9 us -> none
    pallas_call x1, Pallas kernels: 24.3 us -> 23.7 us  [on_device(): pl.pallas_call(functools.partial(kernel, count), out_shape=pltpu.VMEM((2...]
    reshape x0 -> x1, local copies, waits for them, and re-layouts: none -> 0.61 us  [on_device(): return (gradients[:OWN].reshape(-1), gradients[OWN:].reshape(-1))]
where the time goes in v4:
time: 25 us; the launch traced here: 24.9 us
  Pallas kernels  23.7 us (95%)
  between operations  0.64 us (3%)
  local copies, waits for them, and re-layouts  0.61 us (2%)
    pallas_call x1, Pallas kernels, on_device(): pl.pallas_call(functools.partial(kernel, count), out_shape=pltpu.VMEM((2...  23.7 us
    reshape x1, local copies, waits for them, and re-layouts, on_device(): return (gradients[:OWN].reshape(-1), gradients[OWN:].reshape(-1))  0.61 us

profile of v4, /device:TPU:24, one launch (start us, length us, event | category | flops | bytes accessed | tf_op | source)
XLA Modules:
  0.0 24.9 jit_solution(7736575837497604338)
XLA Ops:
  0.6 23.7 %shard_map.131 = f32[32,128]{1,0:T(8,128)S(1)} custom-call(f32[24,2048]{1,0:T(8,128)} %bitcast.22, f32[24,2048]{1,0:T(8,128)} %bitcast.23, f32[8,2048]{1,0:T(8,128)} %press_hbm.1, f32[8,2048]{1,0:T(8,128)} %apress_hbm.1, f32[16,128]{1,0:T(8,128)} %bitcast.25, f32[16,128]{1,0:T(8,128)} %bitcast.26, f32[24,24]{1,0:T(8,128)} %stiff_hbm.1, ...), custom_call_target="tpu_custom_call" | custom-call | tf_op jit(solution)/shard_map/pallas_call | solution.py:554
  24.3 0.6 %slice_bitcast_fusion = (f32[2048]{0:T(1024)}, f32[2048]{0:T(1024)}) fusion(f32[32,128]{1,0:T(8,128)S(1)} %shard_map.131), kind=kLoop, calls=%fused_computation | loop fusion | bytes 32768 | tf_op jit(solution)/shard_map/reshape | solution.py:610

commit v5 on v4

--- a/solution.py
+++ b/solution.py
@@ -100,10 +100,10 @@
     return jnp.concatenate(columns, axis=1)
 
 
-def scatter_rows(marks, value_ref, rows, index_row):
+def scatter_rows(marks, value_ref, rows, index_row, faces=range(8)):
     chunk_iota = lax.broadcasted_iota(jnp.int32, (rows, LANES), 0)
     left = []
-    for s in range(8):
+    for s in faces:
         value = jnp.broadcast_to(value_ref[s : s + 1, :], (rows, LANES))
         chunk = jnp.concatenate([wide(index_row(s)) >> 7] * (rows // 8), axis=0)
         left.append(jnp.where(chunk == chunk_iota, value, 0.0))
@@ -515,17 +515,23 @@
     for slot in range(EDGE_BLOCKS):
         strain(INNER_BLOCKS + slot, edge_state_ref, slot)
 
-    cell_index = lambda s: send_cells_ref[s : s + 1, :]
-    back_marks_ref[...] = lane_marks(place_ref, cell_index)
-    each(-1, lambda j: back_copy(j).wait_recv())
-    edge_ref[0] = jnp.concatenate([back_in[j] for j in range(NB)], axis=0)
-    out_ref[OWN:, :] = gradient_ref[...] + scatter_rows(
-        back_marks_ref[...], edge_ref.at[0], OWN, cell_index
-    )
     each(-1, lambda j: cell_copy(j).wait_send())
     each(-1, lambda j: perm_copy(j).wait_send())
     each(-1, lambda j: node_copy(j).wait_send())
     each(1, lambda j: back_copy(j).wait_send())
+    cell_index = lambda s: send_cells_ref[s : s + 1, :]
+    back_marks_ref[...] = lane_marks(place_ref, cell_index)
+    gradient = gradient_ref[...]
+    for slots in (range(NB - 2), range(NB - 2, NB)):
+        for j in slots:
+            pl.when(on_axis(-OFFSETS[j]))(lambda j=j: back_copy(j).wait_recv())
+        for j in slots:
+            edge_ref[0, j : j + 1, :] = back_in[j]
+        columns = slice(slots[0] * LANES, (slots[-1] + 1) * LANES)
+        gradient = gradient + scatter_rows(
+            back_marks_ref[:, columns], edge_ref.at[0], OWN, cell_index, slots
+        )
+    out_ref[OWN:, :] = gradient
 
 
 def on_device(

time: 25 us -> 24.9 us (level)
  no operation moved by 1% of the time
where the time goes in v5:
time: 24.9 us; the launch traced here: 24.8 us
  Pallas kernels  23.6 us (95%)
  between operations  0.64 us (3%)
  local copies, waits for them, and re-layouts  0.61 us (2%)
    pallas_call x1, Pallas kernels, on_device(): pl.pallas_call(functools.partial(kernel, count), out_shape=pltpu.VMEM((2...  23.6 us
    reshape x1, local copies, waits for them, and re-layouts, on_device(): return (gradients[:OWN].reshape(-1), gradients[OWN:].reshape(-1))  0.61 us

profile of v5, /device:TPU:24, one launch (start us, length us, event | category | flops | bytes accessed | tf_op | source)
XLA Modules:
  0.0 24.8 jit_solution(9601564963411052897)
XLA Ops:
  0.6 23.6 %shard_map.131 = f32[32,128]{1,0:T(8,128)S(1)} custom-call(f32[24,2048]{1,0:T(8,128)} %bitcast.22, f32[24,2048]{1,0:T(8,128)} %bitcast.23, f32[8,2048]{1,0:T(8,128)} %press_hbm.1, f32[8,2048]{1,0:T(8,128)} %apress_hbm.1, f32[16,128]{1,0:T(8,128)} %bitcast.25, f32[16,128]{1,0:T(8,128)} %bitcast.26, f32[24,24]{1,0:T(8,128)} %stiff_hbm.1, ...), custom_call_target="tpu_custom_call" | custom-call | tf_op jit(solution)/shard_map/pallas_call | solution.py:560
  24.2 0.6 %slice_bitcast_fusion = (f32[2048]{0:T(1024)}, f32[2048]{0:T(1024)}) fusion(f32[32,128]{1,0:T(8,128)S(1)} %shard_map.131), kind=kLoop, calls=%fused_computation | loop fusion | bytes 32768 | tf_op jit(solution)/shard_map/reshape | solution.py:616
